TPU v7x, 32 devices: a whole 2x2x4 slice. The times are simulated.
32 devices in a mesh: member: 2 (over y), tile: 4 (over z), lev: 2 (over x), sub: 2 (over core).
Axes of the slice: x: 2, y: 2, z: 4, core: 2. Of those that a mesh axis runs over, the one named last changes fastest.
Arguments:
- increment: float32 [4, 1024, 128], P(('member', 'lev'), ('tile', 'sub')), parts along dimension 0, may hold values from -6 to 6
- residual: float32 [4, 1024, 128], P(('member', 'lev'), ('tile', 'sub')), parts along dimension 0, may hold values from -6 to 6
- direction: float32 [4, 1024, 128], P(('member', 'lev'), ('tile', 'sub')), parts along dimension 0, may hold values from -6 to 6
- wind_u: bfloat16 [4, 1024, 128], P(('member', 'lev'), ('tile', 'sub')), parts along dimension 0, may hold values from -0.3984375 to 0.3984375
- wind_v: bfloat16 [4, 1024, 128], P(('member', 'lev'), ('tile', 'sub')), parts along dimension 0, may hold values from -0.3984375 to 0.3984375
- diffusion: float32 [2], replicated, may hold values from 0.03 to 0.12
- vertical: float32 [2], replicated, may hold values from 0.02 to 0.1
- background_inv: float32 [2], replicated, may hold values from 0.5 to 2
- side_pair: int32 [8, 4], replicated, may hold values from 0 to 31, as said below
- side_flip: int32 [8, 4], replicated, may hold values from 0 to 1, as said below
- obs_column: int32 [512], P(('tile', 'sub')), may hold values from 0 to 131071, as said below
- obs_time: int32 [512], P(('tile', 'sub')), may hold values from 1 to 4
- obs_count: int32 [8], P(('tile', 'sub')), may hold values from 48 to 64, as said below
- jacobian: bfloat16 [512, 2, 616], P(('tile', 'sub'), 'lev'), may hold values from -4 to 4
- error_inv: float32 [616], replicated, may hold values from 0.2 to 5
Outputs:
- increment_new: float32 [4, 1024, 128], P(('member', 'lev'), ('tile', 'sub')), parts along dimension 0
- residual_new: float32 [4, 1024, 128], P(('member', 'lev'), ('tile', 'sub')), parts along dimension 0
- direction_new: float32 [4, 1024, 128], P(('member', 'lev'), ('tile', 'sub')), parts along dimension 0
There are 2 independent parts, one for each index of `member`. A program takes and returns all parts, laid end to end along the dimension named above; an argument that names none is the same for every part. Nothing has to cross between parts.
Inputs may be any that keep to these rules, and one draw needn't show every extreme that they name: side_pair[side_pair[k]] == k for every side k, and side_pair[k] is a side of another panel, so the panels close into one surface joined edge to edge. side_flip is equal on both sides of a pair. `obs_column`: among the live slots of one owner at most 16 name columns of one panel, and every owner reaches 16 for some panel. `obs_count`: some owner has all 64 slots live.
All inputs are finite; a program needn't handle non-finite values.
Results may differ from a plain program's by a relative error of at most 0.0003.
Values sent between devices are 32-bit elements; how exact they have to be, the bound alone decides.
A program may use at most 64 MiB of HBM per device.

v0:
```python
import jax
import jax.numpy as jnp
from jax import lax
from jax.experimental import pallas as pl
from jax.experimental.pallas import tpu as pltpu
import functools
from jax.sharding import PartitionSpec as P

STEPS = 4


def with_halo(block, sides, width):
    for axis, dim in sides:
        count = lax.axis_size(axis)
        forward = [(i, i + 1) for i in range(count - 1)]
        backward = [(target, source) for source, target in forward]
        low = lax.ppermute(
            lax.slice_in_dim(block, block.shape[dim] - width, None, axis=dim), axis, forward
        )
        high = lax.ppermute(lax.slice_in_dim(block, 0, width, axis=dim), axis, backward)
        block = jnp.concatenate([low, block, high], axis=dim)
    return block


def neighbours(strips, pair_rows, flip_rows):
    everyone = lax.all_gather(strips, ("tile", "sub"), axis=0, tiled=True)
    picked = everyone[pair_rows]
    return jnp.where(flip_rows[:, None, None] == 1, picked[:, :, ::-1], picked)


def level_padded(field):
    return with_halo(field, (("lev", 0),), 1)


def body(
    increment,
    residual,
    direction,
    wind_u,
    wind_v,
    diffusion,
    vertical,
    background_inv,
    side_pair,
    side_flip,
    obs_column,
    obs_time,
    obs_count,
    jacobian,
    error_inv,
):
    depth = increment.shape[0]
    width = increment.shape[2]
    slots = obs_column.shape[0]
    panels = lax.axis_size(("tile", "sub"))
    capacity = max(2, (2 * slots + panels - 1) // panels)
    panel = lax.axis_index(("tile", "sub"))
    first_level = lax.axis_index("lev") * depth
    mixing = lax.dynamic_slice_in_dim(diffusion, first_level, depth)[:, None, None]
    blending = lax.dynamic_slice_in_dim(vertical, first_level, depth)[:, None, None]
    prior = lax.dynamic_slice_in_dim(background_inv, first_level, depth)[:, None, None]
    pair_rows = lax.dynamic_index_in_dim(side_pair, panel, 0, keepdims=False)
    flip_rows = lax.dynamic_index_in_dim(side_flip, panel, 0, keepdims=False)
    speed_u = wind_u.astype(jnp.float32)
    speed_v = wind_v.astype(jnp.float32)
    coefs = (
        mixing + 0.5 * speed_u,
        mixing - 0.5 * speed_u,
        mixing + 0.5 * speed_v,
        mixing - 0.5 * speed_v,
    )
    center = 1.0 - 4.0 * mixing - 2.0 * blending

    def forward(field):
        strips = jnp.stack([field[:, 0, :], field[:, -1, :], field[:, :, 0], field[:, :, -1]])
        halos = neighbours(strips, pair_rows, flip_rows)
        north = jnp.concatenate([halos[0][:, None, :], field[:, :-1, :]], axis=1)
        south = jnp.concatenate([field[:, 1:, :], halos[1][:, None, :]], axis=1)
        west = jnp.concatenate([halos[2][:, :, None], field[:, :, :-1]], axis=2)
        east = jnp.concatenate([field[:, :, 1:], halos[3][:, :, None]], axis=2)
        padded = level_padded(field)
        return (
            center * field
            + coefs[0] * north
            + coefs[1] * south
            + coefs[2] * west
            + coefs[3] * east
            + blending * (padded[:-2] + padded[2:])
        )

    def adjoint(field):
        prods = [c * field for c in coefs]
        strips = jnp.stack(
            [prods[0][:, 0, :], prods[1][:, -1, :], prods[2][:, :, 0], prods[3][:, :, -1]]
        )
        halos = neighbours(strips, pair_rows, flip_rows)
        rows_term = jnp.concatenate([prods[0][:, 1:, :], halos[1][:, None, :]], axis=1)
        rows_term = rows_term + jnp.concatenate([halos[0][:, None, :], prods[1][:, :-1, :]], axis=1)
        cols_term = jnp.concatenate([prods[2][:, :, 1:], halos[3][:, :, None]], axis=2)
        cols_term = cols_term + jnp.concatenate([halos[2][:, :, None], prods[3][:, :, :-1]], axis=2)
        padded = level_padded(blending * field)
        return center * field + rows_term + cols_term + padded[:-2] + padded[2:]

    state = direction
    states = []
    for step in range(STEPS):
        state = forward(state)
        states.append(state.reshape(depth, width * width))
    history = jnp.stack(states, axis=0)
    area = width * width
    alive = jnp.arange(slots, dtype=jnp.int32) < obs_count[0]
    targets = obs_column // area
    cells = obs_column % area
    owned = (
        (targets[:, None] == jnp.arange(panels, dtype=jnp.int32)[None, :]) & alive[:, None]
    ).astype(jnp.int32)
    rank = jnp.sum((jnp.cumsum(owned, axis=0) - owned) * owned, axis=1)
    position = jnp.where(alive, targets * capacity + rank, panels * capacity)
    want_cell = (
        jnp.zeros((panels * capacity,), jnp.int32)
        .at[position]
        .set(cells, mode="drop")
        .reshape(panels, capacity)
    )
    want_time = (
        jnp.ones((panels * capacity,), jnp.int32)
        .at[position]
        .set(obs_time, mode="drop")
        .reshape(panels, capacity)
    )
    asked_cell = lax.all_to_all(want_cell, ("tile", "sub"), split_axis=0, concat_axis=0, tiled=True)
    asked_time = lax.all_to_all(want_time, ("tile", "sub"), split_axis=0, concat_axis=0, tiled=True)
    values = history[asked_time - 1, :, asked_cell]
    sent = lax.all_to_all(values, ("tile", "sub"), split_axis=0, concat_axis=0, tiled=True)
    gathered = sent.reshape(panels * capacity, depth)[jnp.minimum(position, panels * capacity - 1)]
    wide = jacobian.astype(jnp.float32)
    partial_value = jnp.einsum("olc,ol->oc", wide, gathered, precision=lax.Precision.HIGHEST)
    departure = lax.psum(partial_value, "lev")
    weighted = departure * error_inv[None, :]
    back = jnp.einsum("olc,oc->ol", wide, weighted, precision=lax.Precision.HIGHEST)
    back = back * alive.astype(jnp.float32)[:, None]
    outgoing = (
        jnp.zeros((panels * capacity, depth), jnp.float32)
        .at[position]
        .set(back, mode="drop")
        .reshape(panels, capacity, depth)
    )
    incoming = lax.all_to_all(outgoing, ("tile", "sub"), split_axis=0, concat_axis=0, tiled=True)
    flat_cell = asked_cell.reshape(panels * capacity)
    flat_time = asked_time.reshape(panels * capacity) - 1
    forcing = (
        jnp.zeros((STEPS, depth, area), jnp.float32)
        .at[flat_time, :, flat_cell]
        .add(incoming.reshape(panels * capacity, depth))
    )
    forcing = forcing.reshape(STEPS, depth, width, width)
    sensitivity = forcing[STEPS - 1]
    for step in range(STEPS - 1, 0, -1):
        sensitivity = adjoint(sensitivity) + forcing[step - 1]
    sensitivity = adjoint(sensitivity)
    image = prior * direction + sensitivity
    norm_old, curvature, cross, square = lax.psum(
        (
            jnp.sum(residual * residual),
            jnp.sum(direction * image),
            jnp.sum(residual * image),
            jnp.sum(image * image),
        ),
        ("tile", "lev", "sub"),
    )
    alpha = norm_old / curvature
    increment_new = increment + alpha * direction
    residual_new = residual - alpha * image
    norm_new = norm_old - 2.0 * alpha * cross + alpha * alpha * square
    direction_new = residual_new + norm_new / norm_old * direction
    return (increment_new, residual_new, direction_new)


MESH = pl.DeviceIdType.MESH
VM = pl.BlockSpec(memory_space=pltpu.VMEM)
SM = pl.BlockSpec(memory_space=pltpu.SMEM)
F32 = jnp.float32
NT = (((1,), (1,)), ((), ()))
TN = (((0,), (0,)), ((), ()))
NN = (((1,), (0,)), ((), ()))
OBS_ROWS = 8


def grid_sizes():
    return lax.axis_size("tile"), lax.axis_size("lev"), lax.axis_size("sub")


def place(flat, tiles, levs, subs):
    return {
        "tile": flat // (levs * subs),
        "lev": (flat // subs) % levs,
        "sub": flat % subs,
    }


def hail(peers):
    barrier = pltpu.get_barrier_semaphore()
    for peer in peers:
        pl.semaphore_signal(barrier, inc=1, device_id=peer, device_id_type=MESH)


def hailed(peers):
    pl.semaphore_wait(pltpu.get_barrier_semaphore(), len(peers))


def group_peers(sizes):
    tiles, levs, subs = sizes
    total = tiles * levs * subs
    me = (lax.axis_index("tile") * levs + lax.axis_index("lev")) * subs + lax.axis_index("sub")
    return [place(lax.rem(me + k, total), *sizes) for k in range(1, total)]


def halves(x):
    high = x.astype(jnp.bfloat16)
    return high, (x - high.astype(F32)).astype(jnp.bfloat16)


def dot2(values, onehot, dims):
    a, b = halves(values)
    return lax.dot_general(a, onehot, dims, preferred_element_type=F32) + lax.dot_general(
        b, onehot, dims, preferred_element_type=F32)


def dot2r(onehot, values, dims):
    a, b = halves(values)
    return lax.dot_general(onehot, a, dims, preferred_element_type=F32) + lax.dot_general(
        onehot, b, dims, preferred_element_type=F32)


def per_level(ref, levels, ndim):
    return jnp.stack([jnp.full((1,) * (ndim - 1), ref[l], F32) for l in range(levels)])


def edge_index(shape, rows, width):
    r = lax.broadcasted_iota(jnp.int32, shape, len(shape) - 2)
    return r if rows == width else jnp.where(r < rows // 2, r, r + (width - rows))


def column_of(halo, rows):
    width = halo.shape[-1]
    shape = (rows, width)
    hit = edge_index(shape, rows, width) == lax.broadcasted_iota(jnp.int32, shape, 1)
    return jnp.sum(jnp.where(hit, halo, 0.0), axis=-1, keepdims=True)


def shifted(x, axis, by, edge):
    n = x.shape[axis]
    rolled = pltpu.roll(x, by % n, axis)
    place_of = lax.broadcasted_iota(jnp.int32, x.shape[-2:], axis - (x.ndim - 2))
    return jnp.where(place_of == (0 if by == 1 else n - 1), edge, rolled)


def vertical_sum(x):
    levels = x.shape[0]
    parts = []
    for l in range(levels):
        total = jnp.zeros_like(x[l])
        if l > 0:
            total = total + x[l - 1]
        if l + 1 < levels:
            total = total + x[l + 1]
        parts.append(total)
    return jnp.stack(parts)


def forward_tile(x, c, center, vert, h):
    r, w = x.ndim - 2, x.ndim - 1
    rows = x.shape[r]
    return (
        center * x
        + c[0] * shifted(x, r, 1, h[0])
        + c[1] * shifted(x, r, -1, h[1])
        + c[2] * shifted(x, w, 1, column_of(h[2], rows))
        + c[3] * shifted(x, w, -1, column_of(h[3], rows))
        + vert * vertical_sum(x)
    )


def adjoint_tile(x, p, center, vert, h):
    r, w = x.ndim - 2, x.ndim - 1
    rows = x.shape[r]
    return (
        center * x
        + shifted(p[0], r, -1, h[1])
        + shifted(p[1], r, 1, h[0])
        + shifted(p[2], w, -1, column_of(h[3], rows))
        + shifted(p[3], w, 1, column_of(h[2], rows))
        + vertical_sum(vert * x)
    )


def swap(q):
    return (q[2], q[3], q[0], q[1])


def pairing_matrix(pair_ref, flip_ref, panels):
    sides = 4 * panels
    pair, turned = pair_ref[...].T, flip_ref[...].T
    code = (pair % 4) * panels + pair // 4 + sides * turned
    code = jnp.concatenate([code[:, k : k + 1] for k in range(4)], axis=0)
    return (code == lax.broadcasted_iota(jnp.int32, (sides, 2 * sides), 1)).astype(jnp.bfloat16)


def reversal(width):
    a = lax.broadcasted_iota(jnp.int32, (width, width), 0)
    b = lax.broadcasted_iota(jnp.int32, (width, width), 1)
    return (a + b == width - 1).astype(jnp.bfloat16)


def exchange(strips, choose, rev):
    levels, panels, _, width = strips[0].shape
    out = []
    for l in range(levels):
        s = jnp.concatenate([strips[k][l].reshape(panels, width) for k in range(4)], axis=0)
        both = jnp.concatenate([s, dot2(s, rev, NN)], axis=0)
        out.append(dot2r(choose, both, NN))
    h = jnp.stack(out)
    return [h[:, k * panels : (k + 1) * panels].reshape(levels, panels, 1, width) for k in range(4)]


def own_halos(h, store, panel):
    out = []
    for k in range(4):
        store[k] = h[k].reshape(store.shape[1:])
    for k in range(4):
        out.append(store[k, :, pl.ds(panel, 1), :])
    return out


def load_tiles(full, bands, dif_ref, ver_ref):
    levels, panels = bands.shape[0], bands.shape[1]
    tips = 2 * STEPS
    fields = {}
    m4, v4 = per_level(dif_ref, levels, 4), per_level(ver_ref, levels, 4)
    m3, v3 = per_level(dif_ref, levels, 3), per_level(ver_ref, levels, 3)

    def coefs(m, u, v):
        return (m + 0.5 * u, m - 0.5 * u, m + 0.5 * v, m - 0.5 * v)

    def band(f, which):
        start = (2 * f + which) * tips
        return bands[:, :, start : start + tips, :]

    ns = coefs(m4, band(1, 0), band(2, 0))
    we = swap(coefs(m4, band(1, 1), band(2, 1)))
    own = coefs(m3, full[:, 1], full[:, 2])
    scal4 = (1.0 - 4.0 * m4 - 2.0 * v4, v4)
    scal3 = (1.0 - 4.0 * m3 - 2.0 * v3, v3)
    return ns, we, own, scal4, scal3, band


def obs_rows(bands, width):
    base = 12 * STEPS
    column = bands[0, :, base, :].astype(jnp.int32)
    when = bands[0, :, base + 1, :].astype(jnp.int32)
    area = width * width
    live = column >= 0
    column = jnp.maximum(column, 0)
    panel = jnp.where(live, column // area, -1)
    cell = column % area
    return panel, cell // width, cell % width, when


def lanes_flat(x, slots):
    rows, width = x.shape
    per = width // slots
    lane = lax.broadcasted_iota(jnp.int32, (1, width), 1) // slots
    parts = []
    for q in range(0, rows, per):
        line = x[q : q + 1]
        for r in range(1, min(per, rows - q)):
            line = jnp.where(lane == r, pltpu.roll(x[q + r : q + r + 1], r * slots, 1), line)
        parts.append(line)
    return jnp.concatenate(parts, axis=1)


def whole_kernel(
    sizes, *refs,
):
    inputs, (img_out, alpha_out, beta_out), held = refs[:14], refs[14:17], refs[17:31]
    whole_steps(sizes, inputs, held, img_out, alpha_out, beta_out, *refs[31:])


def whole_steps(
    sizes, inputs, held, img_out, alpha_out, beta_out, landed,
    full, jall, bands, vall, gall, sall, store,
    fsend, frecv, zsend, zrecv, xsend, xrecv, csend, crecv, jsend, jrecv,
    gsend, grecv, vsend, vrecv, ssend, srecv,
):
    tiles, levs, subs = sizes
    tile, lev, sub = lax.axis_index("tile"), lax.axis_index("lev"), lax.axis_index("sub")
    loads = [
        pltpu.make_async_copy(src, dst, landed.at[k]) for k, (src, dst) in enumerate(zip(inputs, held))
    ]
    for load in loads[:3]:
        load.start()
    flat_peers = group_peers(sizes)
    hail(flat_peers)
    for load in loads[3:]:
        load.start()
    (dir_ref, wu_ref, wv_ref, col_ref, time_ref, count_ref, jac_ref, pair_ref, flip_ref, dif_ref,
     ver_ref, err_ref, inv_ref, res_ref) = held
    panels = tiles * subs
    everyone = panels * levs
    panel = tile * subs + sub
    me = (tile * levs + lev) * subs + sub
    slots = col_ref.shape[1]
    width = dir_ref.shape[2]
    tips = 2 * STEPS
    last = tips - 1
    for f, ref in enumerate((dir_ref, wu_ref, wv_ref)):
        loads[f].wait()
        x = ref[0].astype(F32)
        full[lev, f] = x
        xt = x.T
        rows = 2 * tips * f
        bands[lev, panel, rows : rows + STEPS] = x[:STEPS]
        bands[lev, panel, rows + STEPS : rows + tips] = x[width - STEPS :]
        bands[lev, panel, rows + tips : rows + tips + STEPS] = xt[:STEPS]
        bands[lev, panel, rows + tips + STEPS : rows + 2 * tips] = xt[width - STEPS :]
    base = 6 * tips
    for load in loads[3:6]:
        load.wait()
    alive = lax.broadcasted_iota(jnp.int32, (1, slots), 1) < count_ref[0]
    cols = jnp.where(alive, col_ref[...].astype(F32), -1.0)
    bands[lev, panel, base : base + OBS_ROWS] = jnp.full((OBS_ROWS, width), -1.0, F32)
    bands[lev, panel, base : base + 1, :slots] = cols
    bands[lev, panel, base + 1 : base + 2, :slots] = time_ref[...].astype(F32)
    loads[6].wait()
    jall[lev] = jac_ref[...].astype(F32)
    hailed(flat_peers)
    started = []

    def send(src, dst, ssem, rsem, where):
        copy = pltpu.make_async_remote_copy(
            src_ref=src, dst_ref=dst, send_sem=ssem, recv_sem=rsem,
            device_id=where, device_id_type=MESH)
        copy.start()
        started.append(copy)
        return copy

    def block(m, j):
        return bands.at[lax.rem(lev - m + levs, levs), lax.rem(tile - j + tiles, tiles) * subs + sub]

    arrivals_z, arrivals_x, arrivals_c, arrivals_f, arrivals_j = {}, {}, [], [], []

    def to_subs(m, j):
        for q in range(1, subs):
            arrivals_c.append(send(block(m, j), block(m, j), csend.at[q, m, j], crecv.at[q, m, j],
                                   {"sub": lax.rem(sub + q, subs)}))

    def to_levs(j):
        for m in range(1, levs):
            arrivals_x[m, j] = send(block(0, j), block(0, j), xsend.at[m, j], xrecv.at[m, j],
                                    {"lev": lax.rem(lev + m, levs)})

    for k in range(1, tiles):
        arrivals_z[k] = send(block(0, 0), block(0, 0), zsend.at[k], zrecv.at[k],
                             {"tile": lax.rem(tile + k, tiles)})
    to_levs(0)
    to_subs(0, 0)
    for m in range(1, levs):
        arrivals_f.append(send(full.at[lev], full.at[lev], fsend.at[m], frecv.at[m],
                               {"lev": lax.rem(lev + m, levs)}))
    order = sorted(range(1, tiles), key=lambda k: min(k, tiles - k))
    for k in order:
        arrivals_z[k].wait_recv()
        to_levs(k)
        to_subs(0, k)
    for m in range(1, levs):
        arrivals_j.append(send(jall.at[lev], jall.at[lev], jsend.at[m], jrecv.at[m],
                               {"lev": lax.rem(lev + m, levs)}))
    for load in loads[7:]:
        load.wait()
    choose = pairing_matrix(pair_ref, flip_ref, panels)
    rev = reversal(width)
    for j in [0] + order:
        for m in range(1, levs):
            arrivals_x[m, j].wait_recv()
            to_subs(m, j)
    for copy in arrivals_f + arrivals_c:
        copy.wait_recv()

    ns, we, own, scal4, scal3, band = load_tiles(full, bands, dif_ref, ver_ref)
    x_ns, x_we, x = band(0, 0), band(0, 1), full[:, 0]
    o_panel, o_i, o_j, o_t = obs_rows(bands, width)
    o_panel, o_i, o_j, o_t = [lanes_flat(v, slots) for v in (o_panel, o_i, o_j, o_t)]
    count = o_i.shape[1]
    spots = lax.broadcasted_iota(jnp.int32, (width, count), 0)
    is_i, is_j = spots == o_i, spots == o_j
    mine = is_i & (o_panel == panel)
    mine_i = mine.astype(jnp.bfloat16)
    values = [jnp.zeros(o_i.shape, F32) for _ in range(levs)]
    arrivals_g = []
    partners = []
    for k in range(1, panels):
        flat = lax.rem(panel + k, panels)
        partners.append((k, {"tile": flat // subs, "sub": lax.rem(flat, subs)}))
    for step in range(STEPS):
        strips = (x_ns[:, :, :1], x_ns[:, :, last:], x_we[:, :, :1], x_we[:, :, last:])
        h = exchange(strips, choose, rev)
        ho = own_halos(h, store, panel)
        x = forward_tile(x, own, *scal3, ho)
        if step + 1 < STEPS:
            x_ns, x_we = (
                forward_tile(x_ns, ns, *scal4, h),
                forward_tile(x_we, we, *scal4, swap(h)),
            )
        for l in range(levs):
            picked = dot2(x[l], mine_i, TN)
            got = jnp.sum(jnp.where(is_j, picked, 0.0), axis=0, keepdims=True)
            values[l] = jnp.where(o_t == step + 1, got, values[l])
        if step == STEPS - 2:
            for copy in arrivals_j:
                copy.wait_recv()
            e8 = jnp.broadcast_to(err_ref[...][None, :], (8, err_ref.shape[0]))
            row = 0
            gall[panel] = jnp.zeros(gall.shape[1:], F32)
            for a in range(levs):
                for b in range(a, levs):
                    g = lax.dot_general(
                        e8, jall[a] * jall[b], NT, precision=lax.Precision.HIGHEST,
                        preferred_element_type=F32)
                    gall[panel, row : row + 1, :slots] = g[:1]
                    row += 1
    lines = count // width
    for l in range(levs):
        for q in range(lines):
            vall[panel, l * lines + q : l * lines + q + 1] = values[l][:, q * width : (q + 1) * width]
    arrivals_v = [
        send(vall.at[panel], vall.at[panel], vsend.at[k], vrecv.at[k], where) for k, where in partners
    ]
    arrivals_g = [
        send(gall.at[panel], gall.at[panel], gsend.at[k], grecv.at[k], where) for k, where in partners
    ]
    at_i, at_j = is_i.astype(jnp.bfloat16), is_j.astype(jnp.bfloat16)
    edge = edge_index((tips, count), tips, width)
    on_i = jnp.concatenate([(edge == o_i) & (o_panel == p) for p in range(panels)], axis=0)
    on_j = jnp.concatenate([(edge == o_j) & (o_panel == p) for p in range(panels)], axis=0)
    for copy in arrivals_v + arrivals_g:
        copy.wait_recv()
    total = jnp.sum(vall[...], axis=0)
    columns = [
        jnp.concatenate([total[l * lines + q : l * lines + q + 1] for q in range(lines)], axis=1)
        for l in range(levs)
    ]
    gram = {}
    row = 0
    for a in range(levs):
        for b in range(a, levs):
            gram[a, b] = gram[b, a] = lanes_flat(gall[:, row, :], slots)
            row += 1
    back = []
    for a in range(levs):
        total = gram[a, 0] * columns[0]
        for b in range(1, levs):
            total = total + gram[a, b] * columns[b]
        back.append(jnp.where(o_panel >= 0, total, 0.0))

    def forcing(t):
        parts = [[], [], []]
        for l in range(levs):
            v = jnp.where(o_t == t, back[l], 0.0)
            parts[0].append(dot2(jnp.where(mine, v, 0.0), at_j, NT))
            parts[1].append(dot2(jnp.where(on_i, v, 0.0), at_j, NT).reshape(panels, tips, width))
            parts[2].append(dot2(jnp.where(on_j, v, 0.0), at_i, NT).reshape(panels, tips, width))
        return [jnp.stack(p) for p in parts]

    x, x_ns, x_we = forcing(STEPS)
    for step in range(STEPS - 1, -1, -1):
        p_ns = [c * x_ns for c in ns]
        p_we = [c * x_we for c in we]
        strips = (p_ns[0][:, :, :1], p_ns[1][:, :, last:], p_we[0][:, :, :1], p_we[1][:, :, last:])
        h = exchange(strips, choose, rev)
        ho = own_halos(h, store, panel)
        x = adjoint_tile(x, [c * x for c in own], *scal3, ho)
        if step > 0:
            f = forcing(step)
            x = x + f[0]
            x_ns = adjoint_tile(x_ns, p_ns, *scal4, h) + f[1]
            x_we = adjoint_tile(x_we, p_we, *scal4, swap(h)) + f[2]
    direction = dir_ref[0]
    image = jnp.zeros_like(direction)
    for l in range(levs):
        image = jnp.where(lev == l, x[l] + inv_ref[l] * direction, image)
    res = res_ref[0]
    pairs = ((res, res), (direction, image), (res, image), (image, image))
    sall[me] = jnp.concatenate(
        [jnp.sum(a * b, axis=0, keepdims=True) for a, b in pairs], axis=0)
    arrivals_s = [
        send(sall.at[me], sall.at[me], ssend.at[k], srecv.at[k], where)
        for k, where in enumerate(flat_peers)
    ]
    for copy in arrivals_s:
        copy.wait_recv()
    total = jnp.sum(jnp.sum(sall[...], axis=0), axis=1, keepdims=True)
    old, curvature, cross, square = [total[k : k + 1] for k in range(4)]
    alpha = old / curvature
    new = old - 2.0 * alpha * cross + alpha * alpha * square
    img_out[0] = image
    alpha_out[0] = jnp.broadcast_to(alpha, alpha_out.shape[1:])
    beta_out[0] = jnp.broadcast_to(new / old, beta_out.shape[1:])
    for copy in started:
        copy.wait_send()


def fused_body(
    increment, residual, direction, wind_u, wind_v, diffusion, vertical, background_inv,
    side_pair, side_flip, obs_column, obs_time, obs_count, jacobian, error_inv,
):
    sizes = grid_sizes()
    tiles, levs, subs = sizes
    panels = tiles * subs
    everyone = panels * levs
    width = increment.shape[2]
    slots, _, channels = jacobian.shape
    dma = pltpu.SemaphoreType.DMA
    band_rows = 12 * STEPS + OBS_ROWS
    per = width // slots
    lines = -(-panels // per)
    grams = levs * (levs + 1) // 2
    row = jax.ShapeDtypeStruct((1, 1, width), F32)
    inputs = (
        direction, wind_u, wind_v, obs_column[None, :], obs_time[None, :], obs_count,
        jacobian.reshape(slots, channels), side_pair.T, side_flip.T, diffusion, vertical,
        error_inv, background_inv, residual,
    )
    scalars = (5, 9, 10, 12)
    landing = [
        (pltpu.SMEM if k in scalars else pltpu.VMEM)(x.shape, x.dtype) for k, x in enumerate(inputs)
    ]
    image, alpha, beta = pl.pallas_call(
        functools.partial(whole_kernel, sizes),
        out_shape=(jax.ShapeDtypeStruct(increment.shape, F32), row, row),
        in_specs=[pl.BlockSpec(memory_space=pl.ANY)] * len(inputs),
        out_specs=(VM, VM, VM),
        scratch_shapes=landing + [
            dma((len(inputs),)),
            pltpu.VMEM((levs, 3, width, width), F32),
            pltpu.VMEM((levs, slots, channels), F32),
            pltpu.VMEM((levs, panels, band_rows, width), F32),
            pltpu.VMEM((panels, levs * lines, width), F32),
            pltpu.VMEM((panels, grams, width), F32),
            pltpu.VMEM((everyone, 4, width), F32),
            pltpu.VMEM((4, levs, panels, width), F32),
            dma((levs,)), dma((levs,)),
            dma((tiles,)), dma((tiles,)),
            dma((levs, tiles)), dma((levs, tiles)),
            dma((subs, levs, tiles)), dma((subs, levs, tiles)),
            dma((levs,)), dma((levs,)),
            dma((panels,)), dma((panels,)),
            dma((panels,)), dma((panels,)),
            dma((everyone,)), dma((everyone,)),
        ],
        compiler_params=pltpu.CompilerParams(
            collective_id=0, has_side_effects=True, vmem_limit_bytes=16 * 1024 * 1024),
        name="whole",
    )(*[x if x.size == 1 else pltpu.with_memory_space_constraint(x, pltpu.HBM) for x in inputs])
    left = residual - alpha * image
    return increment + alpha * direction, left, left + beta * direction


def chosen(*args):
    tiles, levs, subs = grid_sizes()
    increment, jacobian = args[0], args[13]
    width = increment.shape[2]
    gathered = tiles * subs * levs * (12 * STEPS + OBS_ROWS) * width * 4
    own = levs * (3 * width * width + jacobian.shape[0] * jacobian.shape[2]) * 4
    fits = (
        increment.shape[0] == 1
        and increment.shape[1] == width
        and width % jacobian.shape[0] == 0
        and (tiles * subs * jacobian.shape[0]) % width == 0
        and width >= 2 * STEPS
        and gathered <= 2 * own
    )
    return fused_body(*args) if fits else body(*args)


def solution(mesh):
    placed = (
        P(("member", "lev"), ("tile", "sub"), None),
        P(("member", "lev"), ("tile", "sub"), None),
        P(("member", "lev"), ("tile", "sub"), None),
        P(("member", "lev"), ("tile", "sub"), None),
        P(("member", "lev"), ("tile", "sub"), None),
        P(),
        P(),
        P(),
        P(),
        P(),
        P(("tile", "sub")),
        P(("tile", "sub")),
        P(("tile", "sub")),
        P(("tile", "sub"), "lev", None),
        P(),
    )
    return jax.shard_map(
        chosen,
        mesh=mesh,
        in_specs=placed,
        out_specs=(
            P(("member", "lev"), ("tile", "sub"), None),
            P(("member", "lev"), ("tile", "sub"), None),
            P(("member", "lev"), ("tile", "sub"), None),
        ),
        check_vma=False,
    )
```

profile of v0, /device:TPU:0, one launch (start us, length us, event | category | flops | bytes accessed | tf_op | source)
XLA Modules:
  0.0 35.1 jit_solution(10827306111229560571)
XLA Ops:
  1.3 0.0 copy-start
  1.3 0.0 copy-start.1
  1.3 0.0 copy-start.2
  1.3 33.1 %whole.1 = (f32[1,128,128]{2,1,0:T(8,128)S(1)}, f32[1,1,128]{2,1,0:T(1,128)S(1)}, f32[1,1,128]{2,1,0:T(1,128)S(1)}) custom-call(f32[1,128,128]{2,1,0:T(8,128)} %refs_0_.1, bf16[1,128,128]{2,1,0:T(8,128)(2,1)} %refs_1_.1, bf16[1,128,128]{2,1,0:T(8,128)(2,1)} %refs_2_.1, s32[1,64]{1,0:T(1,128)} %bitcast.12, s32[1,64]{1,0:T(1,128)} %bitcast.13, ...), custom_call_target="tpu_custom_call" | custom-call | tf_op jit(solution)/shard_map/whole/pallas_call | solution.py:637
  34.4 0.0 copy-done
  34.4 0.0 copy-done.1
  34.4 0.0 copy-done.2
  34.4 0.7 %multiply_add_fusion = (f32[1,128,128]{2,1,0:T(8,128)}, f32[1,128,128]{2,1,0:T(8,128)}, f32[1,128,128]{2,1,0:T(8,128)}) fusion(f32[1,128,128]{2,1,0:T(8,128)S(1)} %copy-done, f32[128]{0:T(128)S(1)} %bitcast.8, f32[1,128,128]{2,1,0:T(8,128)S(1)} %copy-done.1, f32[1,128,128]{2,1,0:T(8,128)S(1)} %get-tuple-element.7, f32[128]{0:T(128)S(1)} %bitcast.7, ...), kind=kLoop, calls=%fused_computation | loop fusion | flops 98304 | bytes 459776 | tf_op jit(solution)/shard_map/add | solution.py:665
Async XLA Ops:
  1.3 33.1 %copy-start = (f32[1,128,128]{2,1,0:T(8,128)S(1)}, f32[1,128,128]{2,1,0:T(8,128)}, u32[]{:S(2)}) copy-start(f32[1,128,128]{2,1,0:T(8,128)} %refs_0_.1) | copy-start | bytes 196612
  1.3 33.1 %copy-start.1 = (f32[1,128,128]{2,1,0:T(8,128)S(1)}, f32[1,128,128]{2,1,0:T(8,128)}, u32[]{:S(2)}) copy-start(f32[1,128,128]{2,1,0:T(8,128)} %refs_13_.1) | copy-start | bytes 196612
  1.3 33.1 %copy-start.2 = (f32[1,128,128]{2,1,0:T(8,128)S(1)}, f32[1,128,128]{2,1,0:T(8,128)}, u32[]{:S(2)}) copy-start(f32[1,128,128]{2,1,0:T(8,128)} %param.15) | copy-start | bytes 196612
where the time goes:
time: 35.3 us; the launch traced here: 35.1 us
  Pallas kernels  33.1 us (94%)
  between operations  1.34 us (4%)
  other arithmetic  0.69 us (2%)
    pallas_call x1, Pallas kernels, fused_body(): pl.pallas_call(functools.partial(whole_kernel, sizes), out_shape=(jax.Sha...  33.1 us

commit v1 on v0

v1 whole, which is shorter than its diff:
```python
import jax
import jax.numpy as jnp
from jax import lax
from jax.experimental import pallas as pl
from jax.experimental.pallas import tpu as pltpu
import functools
from jax.sharding import PartitionSpec as P

STEPS = 4


def with_halo(block, sides, width):
    for axis, dim in sides:
        count = lax.axis_size(axis)
        forward = [(i, i + 1) for i in range(count - 1)]
        backward = [(target, source) for source, target in forward]
        low = lax.ppermute(
            lax.slice_in_dim(block, block.shape[dim] - width, None, axis=dim), axis, forward
        )
        high = lax.ppermute(lax.slice_in_dim(block, 0, width, axis=dim), axis, backward)
        block = jnp.concatenate([low, block, high], axis=dim)
    return block


def neighbours(strips, pair_rows, flip_rows):
    everyone = lax.all_gather(strips, ("tile", "sub"), axis=0, tiled=True)
    picked = everyone[pair_rows]
    return jnp.where(flip_rows[:, None, None] == 1, picked[:, :, ::-1], picked)


def level_padded(field):
    return with_halo(field, (("lev", 0),), 1)


def body(
    increment,
    residual,
    direction,
    wind_u,
    wind_v,
    diffusion,
    vertical,
    background_inv,
    side_pair,
    side_flip,
    obs_column,
    obs_time,
    obs_count,
    jacobian,
    error_inv,
):
    depth = increment.shape[0]
    width = increment.shape[2]
    slots = obs_column.shape[0]
    panels = lax.axis_size(("tile", "sub"))
    capacity = max(2, (2 * slots + panels - 1) // panels)
    panel = lax.axis_index(("tile", "sub"))
    first_level = lax.axis_index("lev") * depth
    mixing = lax.dynamic_slice_in_dim(diffusion, first_level, depth)[:, None, None]
    blending = lax.dynamic_slice_in_dim(vertical, first_level, depth)[:, None, None]
    prior = lax.dynamic_slice_in_dim(background_inv, first_level, depth)[:, None, None]
    pair_rows = lax.dynamic_index_in_dim(side_pair, panel, 0, keepdims=False)
    flip_rows = lax.dynamic_index_in_dim(side_flip, panel, 0, keepdims=False)
    speed_u = wind_u.astype(jnp.float32)
    speed_v = wind_v.astype(jnp.float32)
    coefs = (
        mixing + 0.5 * speed_u,
        mixing - 0.5 * speed_u,
        mixing + 0.5 * speed_v,
        mixing - 0.5 * speed_v,
    )
    center = 1.0 - 4.0 * mixing - 2.0 * blending

    def forward(field):
        strips = jnp.stack([field[:, 0, :], field[:, -1, :], field[:, :, 0], field[:, :, -1]])
        halos = neighbours(strips, pair_rows, flip_rows)
        north = jnp.concatenate([halos[0][:, None, :], field[:, :-1, :]], axis=1)
        south = jnp.concatenate([field[:, 1:, :], halos[1][:, None, :]], axis=1)
        west = jnp.concatenate([halos[2][:, :, None], field[:, :, :-1]], axis=2)
        east = jnp.concatenate([field[:, :, 1:], halos[3][:, :, None]], axis=2)
        padded = level_padded(field)
        return (
            center * field
            + coefs[0] * north
            + coefs[1] * south
            + coefs[2] * west
            + coefs[3] * east
            + blending * (padded[:-2] + padded[2:])
        )

    def adjoint(field):
        prods = [c * field for c in coefs]
        strips = jnp.stack(
            [prods[0][:, 0, :], prods[1][:, -1, :], prods[2][:, :, 0], prods[3][:, :, -1]]
        )
        halos = neighbours(strips, pair_rows, flip_rows)
        rows_term = jnp.concatenate([prods[0][:, 1:, :], halos[1][:, None, :]], axis=1)
        rows_term = rows_term + jnp.concatenate([halos[0][:, None, :], prods[1][:, :-1, :]], axis=1)
        cols_term = jnp.concatenate([prods[2][:, :, 1:], halos[3][:, :, None]], axis=2)
        cols_term = cols_term + jnp.concatenate([halos[2][:, :, None], prods[3][:, :, :-1]], axis=2)
        padded = level_padded(blending * field)
        return center * field + rows_term + cols_term + padded[:-2] + padded[2:]

    state = direction
    states = []
    for step in range(STEPS):
        state = forward(state)
        states.append(state.reshape(depth, width * width))
    history = jnp.stack(states, axis=0)
    area = width * width
    alive = jnp.arange(slots, dtype=jnp.int32) < obs_count[0]
    targets = obs_column // area
    cells = obs_column % area
    owned = (
        (targets[:, None] == jnp.arange(panels, dtype=jnp.int32)[None, :]) & alive[:, None]
    ).astype(jnp.int32)
    rank = jnp.sum((jnp.cumsum(owned, axis=0) - owned) * owned, axis=1)
    position = jnp.where(alive, targets * capacity + rank, panels * capacity)
    want_cell = (
        jnp.zeros((panels * capacity,), jnp.int32)
        .at[position]
        .set(cells, mode="drop")
        .reshape(panels, capacity)
    )
    want_time = (
        jnp.ones((panels * capacity,), jnp.int32)
        .at[position]
        .set(obs_time, mode="drop")
        .reshape(panels, capacity)
    )
    asked_cell = lax.all_to_all(want_cell, ("tile", "sub"), split_axis=0, concat_axis=0, tiled=True)
    asked_time = lax.all_to_all(want_time, ("tile", "sub"), split_axis=0, concat_axis=0, tiled=True)
    values = history[asked_time - 1, :, asked_cell]
    sent = lax.all_to_all(values, ("tile", "sub"), split_axis=0, concat_axis=0, tiled=True)
    gathered = sent.reshape(panels * capacity, depth)[jnp.minimum(position, panels * capacity - 1)]
    wide = jacobian.astype(jnp.float32)
    partial_value = jnp.einsum("olc,ol->oc", wide, gathered, precision=lax.Precision.HIGHEST)
    departure = lax.psum(partial_value, "lev")
    weighted = departure * error_inv[None, :]
    back = jnp.einsum("olc,oc->ol", wide, weighted, precision=lax.Precision.HIGHEST)
    back = back * alive.astype(jnp.float32)[:, None]
    outgoing = (
        jnp.zeros((panels * capacity, depth), jnp.float32)
        .at[position]
        .set(back, mode="drop")
        .reshape(panels, capacity, depth)
    )
    incoming = lax.all_to_all(outgoing, ("tile", "sub"), split_axis=0, concat_axis=0, tiled=True)
    flat_cell = asked_cell.reshape(panels * capacity)
    flat_time = asked_time.reshape(panels * capacity) - 1
    forcing = (
        jnp.zeros((STEPS, depth, area), jnp.float32)
        .at[flat_time, :, flat_cell]
        .add(incoming.reshape(panels * capacity, depth))
    )
    forcing = forcing.reshape(STEPS, depth, width, width)
    sensitivity = forcing[STEPS - 1]
    for step in range(STEPS - 1, 0, -1):
        sensitivity = adjoint(sensitivity) + forcing[step - 1]
    sensitivity = adjoint(sensitivity)
    image = prior * direction + sensitivity
    norm_old, curvature, cross, square = lax.psum(
        (
            jnp.sum(residual * residual),
            jnp.sum(direction * image),
            jnp.sum(residual * image),
            jnp.sum(image * image),
        ),
        ("tile", "lev", "sub"),
    )
    alpha = norm_old / curvature
    increment_new = increment + alpha * direction
    residual_new = residual - alpha * image
    norm_new = norm_old - 2.0 * alpha * cross + alpha * alpha * square
    direction_new = residual_new + norm_new / norm_old * direction
    return (increment_new, residual_new, direction_new)


MESH = pl.DeviceIdType.MESH
VM = pl.BlockSpec(memory_space=pltpu.VMEM)
F32 = jnp.float32
BF16 = jnp.bfloat16
NT = (((1,), (1,)), ((), ()))
TN = (((0,), (0,)), ((), ()))
NN = (((1,), (0,)), ((), ()))
FACTS = 3
MARGIN = 8
INPUTS = 14


def grid_sizes():
    return lax.axis_size("tile"), lax.axis_size("lev"), lax.axis_size("sub")


def slot_capacity(slots, panels):
    return max(2, (2 * slots + panels - 1) // panels)


def place(flat, tiles, levs, subs):
    return {
        "tile": flat // (levs * subs),
        "lev": (flat // subs) % levs,
        "sub": flat % subs,
    }


def hail(peers):
    barrier = pltpu.get_barrier_semaphore()
    for peer in peers:
        pl.semaphore_signal(barrier, inc=1, device_id=peer, device_id_type=MESH)


def hailed(peers):
    pl.semaphore_wait(pltpu.get_barrier_semaphore(), len(peers))


def group_peers(sizes):
    tiles, levs, subs = sizes
    total = tiles * levs * subs
    me = (lax.axis_index("tile") * levs + lax.axis_index("lev")) * subs + lax.axis_index("sub")
    return [place(lax.rem(me + k, total), *sizes) for k in range(1, total)]


def dot(a, b, dims, precision=None):
    return lax.dot_general(a, b, dims, precision=precision, preferred_element_type=F32)


def iota(shape, axis):
    return lax.broadcasted_iota(jnp.int32, shape, axis)


def fiota(shape, axis):
    return iota(shape, axis).astype(F32)


def halves(x):
    high = x.astype(BF16).astype(F32)
    return high, x - high


def per_level(ref, levels, ndim):
    return jnp.stack([jnp.full((1,) * (ndim - 1), ref[l], F32) for l in range(levels)])


def edge_index(shape, rows, width):
    r = iota(shape, len(shape) - 2)
    return jnp.where(r < rows // 2, r, r + (width - rows))


def column_of(halo, hit):
    return jnp.sum(jnp.where(hit, halo, 0.0), axis=-1, keepdims=True)


def shifted(x, axis, by, edge):
    n = x.shape[axis]
    rolled = pltpu.roll(x, by % n, axis)
    place_of = iota(x.shape[-2:], axis - (x.ndim - 2))
    return jnp.where(place_of == (0 if by == 1 else n - 1), edge, rolled)


def vertical_sum(x):
    levels = x.shape[0]
    parts = []
    for l in range(levels):
        total = jnp.zeros_like(x[l])
        if l > 0:
            total = total + x[l - 1]
        if l + 1 < levels:
            total = total + x[l + 1]
        parts.append(total)
    return jnp.stack(parts)


def forward_tile(x, c, center, vert, h, hit):
    r, w = x.ndim - 2, x.ndim - 1
    return (
        center * x
        + c[0] * shifted(x, r, 1, h[0])
        + c[1] * shifted(x, r, -1, h[1])
        + c[2] * shifted(x, w, 1, column_of(h[2], hit))
        + c[3] * shifted(x, w, -1, column_of(h[3], hit))
        + vert * vertical_sum(x)
    )


def adjoint_tile(x, p, center, vert, h, hit):
    r, w = x.ndim - 2, x.ndim - 1
    return (
        center * x
        + shifted(p[0], r, -1, h[1])
        + shifted(p[1], r, 1, h[0])
        + shifted(p[2], w, -1, column_of(h[3], hit))
        + shifted(p[3], w, 1, column_of(h[2], hit))
        + vertical_sum(vert * x)
    )


def swap(q):
    return (q[2], q[3], q[0], q[1])


def pairing_matrix(pair_ref, flip_ref, panels):
    sides = 4 * panels
    pair, turned = pair_ref[...].T, flip_ref[...].T
    code = (pair % 4) * panels + pair // 4 + sides * turned
    code = jnp.concatenate([code[:, k : k + 1] for k in range(4)], axis=0)
    shape = (sides, 2 * sides)
    picks = code == iota(shape, 1)
    return jnp.concatenate([picks.astype(F32)] * 2, axis=1).astype(BF16)


def reversal(width):
    shape = (2 * width, width)
    a = iota(shape, 0)
    a = jnp.where(a < width, a, a - width)
    return (a + iota(shape, 1) == width - 1).astype(BF16)


def exchange(strips, choose, rev):
    levels, panels, _, width = strips[0].shape
    sides = 4 * panels
    s = jnp.concatenate(
        [strips[k][l].reshape(panels, width) for l in range(levels) for k in range(4)], axis=0)
    high, low = halves(s)
    turned = dot(jnp.concatenate([high, low], axis=1).astype(BF16), rev, NN)
    thigh, tlow = halves(turned)
    both = jnp.concatenate(
        [
            jnp.concatenate([v[l * sides : (l + 1) * sides] for v in (high, thigh, low, tlow)], axis=0)
            for l in range(levels)
        ], axis=1)
    h = dot(choose, both.astype(BF16), NN)
    return [
        jnp.stack([
            h[k * panels : (k + 1) * panels, l * width : (l + 1) * width] for l in range(levels)
        ]).reshape(levels, panels, 1, width)
        for k in range(4)
    ]


def own_halos(h, store, panel):
    for k in range(4):
        store[k] = h[k].reshape(store.shape[1:])
    return [store[k, :, pl.ds(panel, 1), :] for k in range(4)]


def slot_rows(col, when, count, panels, area, width, capacity):
    slots = col.shape[1]
    alive = iota((1, slots), 1) < count
    panel = jnp.where(alive, col // area, -1)
    cell = col % area
    owned = (iota((panels, slots), 0) == panel).astype(F32)
    earlier = (iota((slots, slots), 0) < iota((slots, slots), 1)).astype(BF16)
    rank = jnp.sum(owned * dot(owned.astype(BF16), earlier, NN), axis=0, keepdims=True)
    slot = jnp.where(alive, panel.astype(F32) * capacity + rank, -1.0)
    spread = (fiota((panels * capacity, slots), 0) == slot).astype(BF16)
    facts = jnp.concatenate([cell // width + 1, cell % width + 1, when], axis=0).astype(F32)
    facts = jnp.concatenate([facts, jnp.zeros((8 - FACTS, slots), F32)], axis=0)
    return dot(facts.astype(BF16), spread, NT), spread


def by_panel(a, capacity):
    owners, width = a.shape
    mine = iota((owners, width), 1) // capacity == iota((owners, width), 0)
    slanted = pltpu.roll(a, 0, 1, stride=capacity, stride_axis=0)
    rows = []
    for p in range(width // capacity):
        r = pltpu.roll(slanted, width - p * capacity, 1) if p else slanted
        rows.append(jnp.sum(jnp.where(mine, r, 0.0), axis=0, keepdims=True))
    return jnp.concatenate(rows, axis=0)


def whole_kernel(sizes, capacity, *refs):
    tiles, levs, subs = sizes
    inputs, (img_out, alpha_out, beta_out) = refs[:INPUTS], refs[INPUTS : INPUTS + 3]
    held = refs[INPUTS + 3 : 2 * INPUTS + 3]
    (landed, stage, win, bands, jmine, jother, gall, vall, sall, rother, isent, igot, store, box,
     fsend, frecv, zsend, zrecv, xsend, xrecv, csend, crecv, jsend, jrecv, rsend, rrecv, isend, irecv,
     gsend, grecv, vsend, vrecv, ssend, srecv) = refs[2 * INPUTS + 3 :]
    (dir_ref, wu_ref, wv_ref, col_ref, time_ref, count_ref, jac_ref, err_ref, pair_ref, flip_ref,
     dif_ref, ver_ref, inv_ref, res_ref) = held
    loads = [
        pltpu.make_async_copy(src, dst, landed.at[k]) for k, (src, dst) in enumerate(zip(inputs, held))
    ]
    for load in loads[:6]:
        load.start()
    flat_peers = group_peers(sizes)
    hail(flat_peers)
    for load in loads[6:]:
        load.start()

    tile, lev, sub = lax.axis_index("tile"), lax.axis_index("lev"), lax.axis_index("sub")
    panels = tiles * subs
    panel = tile * subs + sub
    me = (tile * levs + lev) * subs + sub
    other = 1 - lev
    slots, channels = jac_ref.shape
    width = dir_ref.shape[2]
    area = width * width
    tips = 2 * STEPS
    last = tips - 1
    base = 6 * tips
    half = width // levs
    rows = half + MARGIN
    start = pl.multiple_of(lev * (width - rows), MARGIN)
    ostart = pl.multiple_of(other * (width - rows), MARGIN)
    mid = pl.multiple_of(lev * half, MARGIN)
    omid = pl.multiple_of(other * half, MARGIN)
    share = slots // levs

    for f, ref in enumerate((dir_ref, wu_ref, wv_ref)):
        loads[f].wait()
        x = ref[0].astype(F32)
        stage[f] = x
        xt = x.T
        at = 2 * tips * f
        bands[lev, panel, at : at + STEPS] = x[:STEPS]
        bands[lev, panel, at + STEPS : at + tips] = x[width - STEPS :]
        bands[lev, panel, at + tips : at + tips + STEPS] = xt[:STEPS]
        bands[lev, panel, at + tips + STEPS : at + 2 * tips] = xt[width - STEPS :]
    for load in loads[3:6]:
        load.wait()
    facts, spread = slot_rows(
        col_ref[...], time_ref[...], count_ref[0], panels, area, width, capacity)
    bands[lev, panel, base : base + FACTS] = facts[:FACTS]
    hailed(flat_peers)
    started = []

    def send(src, dst, ssem, rsem, where):
        copy = pltpu.make_async_remote_copy(
            src_ref=src, dst_ref=dst, send_sem=ssem, recv_sem=rsem,
            device_id=where, device_id_type=MESH)
        copy.start()
        started.append(copy)
        return copy

    def block(m, j):
        return bands.at[lax.rem(lev - m + levs, levs), lax.rem(tile - j + tiles, tiles) * subs + sub]

    arrivals_z, arrivals_x, arrivals_c = {}, {}, []
    across = {"lev": other}

    def to_subs(m, j):
        for q in range(1, subs):
            arrivals_c.append(send(block(m, j), block(m, j), csend.at[q, m, j], crecv.at[q, m, j],
                                   {"sub": lax.rem(sub + q, subs)}))

    def to_lev(j):
        arrivals_x[j] = send(block(0, j), block(0, j), xsend.at[j], xrecv.at[j], across)

    order = sorted(range(1, tiles), key=lambda k: min(k, tiles - k))
    for k in order:
        arrivals_z[k] = send(block(0, 0), block(0, 0), zsend.at[k], zrecv.at[k],
                             {"tile": lax.rem(tile + k, tiles)})
    to_lev(0)
    to_subs(0, 0)
    fields = send(stage.at[:, pl.ds(ostart, rows)], win.at[lev], fsend, frecv, across)
    for f in range(3):
        win[lev, f] = stage[f, pl.ds(start, rows)]
    for load in loads[6:]:
        load.wait()
    jmine[...] = jac_ref[...].astype(F32)
    choose = pairing_matrix(pair_ref, flip_ref, panels)
    rev = reversal(width)
    e8 = jnp.broadcast_to(err_ref[...][None, :], (8, channels))
    high = lax.Precision.HIGHEST

    def slotted(g):
        a, b = halves(g)
        both = jnp.concatenate([a, b], axis=0).astype(BF16)
        out = dot(both, spread, NT)
        return out[:1] + out[8:9]

    gall[lev, panel, 0:1] = slotted(dot(e8, jmine[...] * jmine[...], NT, high))
    for k in order:
        arrivals_z[k].wait_recv()
        to_lev(k)
        to_subs(0, k)
    jcopy = send(jmine.at[pl.ds(pl.multiple_of(other * share, MARGIN), share)], jother, jsend, jrecv, across)
    rcopy = send(res_ref.at[0, pl.ds(omid, half)], rother, rsend, rrecv, across)
    for j in [0] + order:
        arrivals_x[j].wait_recv()
        to_subs(1, j)
    for copy in [fields] + arrivals_c:
        copy.wait_recv()

    def band(f, which):
        at = (2 * f + which) * tips
        return bands[:, :, at : at + tips, :]

    def coefs(m, u, v):
        return (m + 0.5 * u, m - 0.5 * u, m + 0.5 * v, m - 0.5 * v)

    m4, v4 = per_level(dif_ref, levs, 4), per_level(ver_ref, levs, 4)
    m3, v3 = per_level(dif_ref, levs, 3), per_level(ver_ref, levs, 3)
    ns = coefs(m4, band(1, 0), band(2, 0))
    we = swap(coefs(m4, band(1, 1), band(2, 1)))
    own = coefs(m3, win[:, 1], win[:, 2])
    scal4 = (1.0 - 4.0 * m4 - 2.0 * v4, v4)
    scal3 = (1.0 - 4.0 * m3 - 2.0 * v3, v3)
    hit4 = edge_index((tips, width), tips, width) == iota((tips, width), 1)
    hit3 = iota((rows, width), 0) + start == iota((rows, width), 1)
    x_ns, x_we, x = band(0, 0), band(0, 1), win[:, 0]

    o_i, o_j, o_t = [by_panel(bands[0, :, base + k, :], capacity) for k in range(FACTS)]
    for k, v in enumerate((o_i, o_j, o_t)):
        box[k] = v
    s_i, s_j, s_t = [box[k, pl.ds(panel, 1), :] for k in range(FACTS)]
    line = iota((rows, width), 0)
    mine = (line + start + 1).astype(F32) == s_i
    inside = jnp.where((line >= lev * MARGIN) & (line < lev * MARGIN + half), 1.0, 0.0)
    here = jnp.where(mine, inside, 0.0)
    picked = [None] * levs
    for step in range(STEPS):
        strips = (x_ns[:, :, :1], x_ns[:, :, last:], x_we[:, :, :1], x_we[:, :, last:])
        h = exchange(strips, choose, rev)
        ho = own_halos(h, store.at[step % 2], panel)
        x = forward_tile(x, own, *scal3, ho, hit3)
        if step + 1 < STEPS:
            x_ns, x_we = (
                forward_tile(x_ns, ns, *scal4, h, hit4),
                forward_tile(x_we, we, *scal4, swap(h), hit4),
            )
        now = jnp.where(s_t == step + 1.0, here, 0.0)
        now = jnp.concatenate([now, now], axis=0).astype(BF16)
        for l in range(levs):
            got = dot(jnp.concatenate(halves(x[l]), axis=0).astype(BF16), now, TN)
            picked[l] = got if picked[l] is None else picked[l] + got
        if step == 1:
            jcopy.wait_recv()
            cross = dot(e8, jmine[pl.ds(pl.multiple_of(lev * share, MARGIN), share)] * jother[...], NT, high)
            cross = jnp.concatenate([cross] * levs, axis=1)
            cross = jnp.where(iota(cross.shape, 1) // share == lev, cross, 0.0)
            gall[lev, panel, 1:2] = slotted(cross)
            arrivals_g = [
                send(gall.at[lev, panel], gall.at[lev, panel], gsend.at[k], grecv.at[k], where)
                for k, where in enumerate(flat_peers)
            ]
    at_j = fiota((width, width), 0) + 1.0 == s_j
    for l in range(levs):
        vall[lev, panel, l : l + 1] = jnp.sum(jnp.where(at_j, picked[l], 0.0), axis=0, keepdims=True)
    arrivals_v = [
        send(vall.at[lev, panel], vall.at[lev, panel], vsend.at[k], vrecv.at[k], where)
        for k, where in enumerate(flat_peers)
    ]

    edge = edge_index((tips, width), tips, width).astype(F32) + 1.0
    spots = fiota((width, width), 0) + 1.0

    def onehots(p, a, b):
        tip = jnp.concatenate(
            [jnp.where((edge == a[p : p + 1]) & (o_t[p : p + 1] == t), 1.0, 0.0)
             for t in range(1, STEPS + 1)], axis=0)
        along = jnp.where(spots == b[p : p + 1], 1.0, 0.0)
        return tip, jnp.concatenate([along, along], axis=1).astype(BF16)

    hot_ns = [onehots(p, o_i, o_j) for p in range(panels)]
    hot_we = [onehots(p, o_j, o_i) for p in range(panels)]
    rows_own = jnp.concatenate(
        [jnp.where(mine & (s_t == t), 1.0, 0.0) for t in range(1, STEPS + 1)], axis=0)
    rows_own = jnp.concatenate([rows_own, rows_own], axis=1).astype(BF16)
    for copy in arrivals_g:
        copy.wait_recv()
    gram = {(l, l): by_panel(gall[l, :, 0, :], capacity) for l in range(levs)}
    gram[0, 1] = gram[1, 0] = by_panel(gall[0, :, 1, :] + gall[1, :, 1, :], capacity)
    for copy in arrivals_v:
        copy.wait_recv()
    total = vall[0] + vall[1]
    back = [gram[a, 0] * total[:, 0] + gram[a, 1] * total[:, 1] for a in range(levs)]
    parts = [halves(b) for b in back]

    def band_forcing(hot):
        out = []
        for p in range(panels):
            tip, along = hot[p]
            left = jnp.concatenate(
                [jnp.concatenate([tip * v[p : p + 1] for v in parts[l]], axis=1) for l in range(levs)],
                axis=0)
            out.append(dot(left.astype(BF16), along, NT))
        return [
            jnp.stack([
                jnp.stack([o[(l * STEPS + t) * tips : (l * STEPS + t + 1) * tips] for o in out])
                for l in range(levs)])
            for t in range(STEPS)
        ]

    for l in range(levs):
        box[l] = back[l]
    scaled = []
    for l in range(levs):
        v = halves(box[l, pl.ds(panel, 1), :])
        scaled.append(jnp.concatenate([jnp.where(at_j, w, 0.0) for w in v], axis=1))
    flat = dot(rows_own, jnp.concatenate(scaled, axis=0).astype(BF16), NT)
    force = [
        jnp.stack([flat[t * rows : (t + 1) * rows, l * width : (l + 1) * width] for l in range(levs)])
        for t in range(STEPS)
    ]
    force_ns, force_we = band_forcing(hot_ns), band_forcing(hot_we)
    x, x_ns, x_we = force[-1], force_ns[-1], force_we[-1]
    for step in range(STEPS - 1, -1, -1):
        p_ns = [c * x_ns for c in ns]
        p_we = [c * x_we for c in we]
        strips = (p_ns[0][:, :, :1], p_ns[1][:, :, last:], p_we[0][:, :, :1], p_we[1][:, :, last:])
        h = exchange(strips, choose, rev)
        ho = own_halos(h, store.at[step % 2], panel)
        x = adjoint_tile(x, [c * x for c in own], *scal3, ho, hit3)
        if step > 0:
            x = x + force[step - 1]
            x_ns = adjoint_tile(x_ns, p_ns, *scal4, h, hit4) + force_ns[step - 1]
            x_we = adjoint_tile(x_we, p_we, *scal4, swap(h), hit4) + force_we[step - 1]

    rcopy.wait_recv()
    x = jnp.where(lev == 0, x[:, :half], x[:, rows - half :])
    direction = [win[l, 0, pl.ds(pl.multiple_of(lev * MARGIN, MARGIN), half)] for l in range(levs)]
    image = [x[l] + inv_ref[l] * direction[l] for l in range(levs)]
    own_res, other_res = res_ref[0, pl.ds(mid, half)], rother[...]
    sums = None
    for l in range(levs):
        res = jnp.where(lev == l, own_res, other_res)
        pairs = ((res, res), (direction[l], image[l]), (res, image[l]), (image[l], image[l]))
        part = jnp.concatenate([jnp.sum(a * b, axis=0, keepdims=True) for a, b in pairs], axis=0)
        sums = part if sums is None else sums + part
    sall[me] = sums
    arrivals_s = [
        send(sall.at[me], sall.at[me], ssend.at[k], srecv.at[k], where)
        for k, where in enumerate(flat_peers)
    ]
    isent[...] = jnp.where(lev == 0, image[1], image[0])
    icopy = send(isent, igot, isend, irecv, across)
    img_out[0, pl.ds(mid, half)] = jnp.where(lev == 0, image[0], image[1])
    icopy.wait_recv()
    img_out[0, pl.ds(omid, half)] = igot[...]
    for copy in arrivals_s:
        copy.wait_recv()
    total = jnp.sum(jnp.sum(sall[...], axis=0), axis=1, keepdims=True)
    old, curvature, cross, square = [total[k : k + 1] for k in range(4)]
    alpha = old / curvature
    new = old - 2.0 * alpha * cross + alpha * alpha * square
    alpha_out[0] = jnp.broadcast_to(alpha, alpha_out.shape[1:])
    beta_out[0] = jnp.broadcast_to(new / old, beta_out.shape[1:])
    for copy in started:
        copy.wait_send()


def fused_body(
    increment, residual, direction, wind_u, wind_v, diffusion, vertical, background_inv,
    side_pair, side_flip, obs_column, obs_time, obs_count, jacobian, error_inv,
):
    sizes = grid_sizes()
    tiles, levs, subs = sizes
    panels = tiles * subs
    everyone = panels * levs
    width = increment.shape[2]
    slots, _, channels = jacobian.shape
    half = width // levs
    rows = half + MARGIN
    dma = pltpu.SemaphoreType.DMA
    inputs = (
        direction, wind_u, wind_v, obs_column[None, :], obs_time[None, :], obs_count,
        jacobian.reshape(slots, channels), error_inv, side_pair.T, side_flip.T, diffusion, vertical,
        background_inv, residual,
    )
    scalars = (5, 10, 11, 12)
    landing = [
        (pltpu.SMEM if k in scalars else pltpu.VMEM)(x.shape, x.dtype) for k, x in enumerate(inputs)
    ]
    row = jax.ShapeDtypeStruct((1, 1, width), F32)
    image, alpha, beta = pl.pallas_call(
        functools.partial(whole_kernel, sizes, slot_capacity(slots, panels)),
        out_shape=(jax.ShapeDtypeStruct(increment.shape, F32), row, row),
        in_specs=[pl.BlockSpec(memory_space=pl.ANY)] * len(inputs),
        out_specs=(VM, VM, VM),
        scratch_shapes=landing + [
            dma((len(inputs),)),
            pltpu.VMEM((3, width, width), F32),
            pltpu.VMEM((levs, 3, rows, width), F32),
            pltpu.VMEM((levs, panels, 12 * STEPS + FACTS, width), F32),
            pltpu.VMEM((slots, channels), F32),
            pltpu.VMEM((slots // levs, channels), F32),
            pltpu.VMEM((levs, panels, 2, width), F32),
            pltpu.VMEM((levs, panels, levs, width), F32),
            pltpu.VMEM((everyone, 4, width), F32),
            pltpu.VMEM((half, width), F32),
            pltpu.VMEM((half, width), F32),
            pltpu.VMEM((half, width), F32),
            pltpu.VMEM((2, 4, levs, panels, width), F32),
            pltpu.VMEM((FACTS, panels, width), F32),
            dma, dma,
            dma((tiles,)), dma((tiles,)),
            dma((tiles,)), dma((tiles,)),
            dma((subs, levs, tiles)), dma((subs, levs, tiles)),
            dma, dma,
            dma, dma,
            dma, dma,
            dma((everyone,)), dma((everyone,)),
            dma((everyone,)), dma((everyone,)),
            dma((everyone,)), dma((everyone,)),
        ],
        compiler_params=pltpu.CompilerParams(
            collective_id=0, has_side_effects=True, vmem_limit_bytes=16 * 1024 * 1024),
        name="whole",
    )(*[x if x.size == 1 else pltpu.with_memory_space_constraint(x, pltpu.HBM) for x in inputs])
    left = residual - alpha * image
    return increment + alpha * direction, left, left + beta * direction


def chosen(*args):
    tiles, levs, subs = grid_sizes()
    increment, jacobian = args[0], args[13]
    width, slots, panels = increment.shape[2], jacobian.shape[0], tiles * subs
    fits = (
        levs == 2
        and increment.shape[0] == 1
        and increment.shape[1] == width
        and panels * slot_capacity(slots, panels) == width
        and panels == 8
        and slots % (8 * levs) == 0
        and width % (8 * levs) == 0
        and STEPS <= MARGIN
        and width >= 2 * STEPS
    )
    return fused_body(*args) if fits else body(*args)


def solution(mesh):
    placed = (
        P(("member", "lev"), ("tile", "sub"), None),
        P(("member", "lev"), ("tile", "sub"), None),
        P(("member", "lev"), ("tile", "sub"), None),
        P(("member", "lev"), ("tile", "sub"), None),
        P(("member", "lev"), ("tile", "sub"), None),
        P(),
        P(),
        P(),
        P(),
        P(),
        P(("tile", "sub")),
        P(("tile", "sub")),
        P(("tile", "sub")),
        P(("tile", "sub"), "lev", None),
        P(),
    )
    return jax.shard_map(
        chosen,
        mesh=mesh,
        in_specs=placed,
        out_specs=(
            P(("member", "lev"), ("tile", "sub"), None),
            P(("member", "lev"), ("tile", "sub"), None),
            P(("member", "lev"), ("tile", "sub"), None),
        ),
        check_vma=False,
    )
```

time: 35.3 us -> 31.2 us (0.88)
  Pallas kernels: 33.1 us -> 29 us
    pallas_call x1, Pallas kernels: 33.1 us -> 29 us  [fused_body(): pl.pallas_call(functools.partial(whole_kernel, sizes, slot_capacity(slots...]
where the time goes in v1:
time: 31.2 us; the launch traced here: 31.1 us
  Pallas kernels  29 us (93%)
  between operations  1.34 us (4%)
  other arithmetic  0.69 us (2%)
    pallas_call x1, Pallas kernels, fused_body(): pl.pallas_call(functools.partial(whole_kernel, sizes, slot_capacity(slots...  29 us
    add x1, other arithmetic, fused_body(): return (increment + alpha * direction, left, left + beta * direction)  0.69 us

profile of v1, /device:TPU:0, one launch (start us, length us, event | category | flops | bytes accessed | tf_op | source)
XLA Modules:
  0.0 31.1 jit_solution(182359285550242100)
XLA Ops:
  1.3 0.0 copy-start
  1.3 0.0 copy-start.1
  1.3 0.0 copy-start.2
  1.3 29.0 %whole.1 = (f32[1,128,128]{2,1,0:T(8,128)S(1)}, f32[1,1,128]{2,1,0:T(1,128)S(1)}, f32[1,1,128]{2,1,0:T(1,128)S(1)}) custom-call(f32[1,128,128]{2,1,0:T(8,128)} %refs_0_.1, bf16[1,128,128]{2,1,0:T(8,128)(2,1)} %refs_1_.1, bf16[1,128,128]{2,1,0:T(8,128)(2,1)} %refs_2_.1, s32[1,64]{1,0:T(1,128)} %bitcast.12, s32[1,64]{1,0:T(1,128)} %bitcast.13, ...), custom_call_target="tpu_custom_call" | custom-call | tf_op jit(solution)/shard_map/whole/pallas_call | solution.py:668
  30.3 0.0 copy-done
  30.4 0.0 copy-done.1
  30.4 0.0 copy-done.2
  30.4 0.7 %multiply_add_fusion = (f32[1,128,128]{2,1,0:T(8,128)}, f32[1,128,128]{2,1,0:T(8,128)}, f32[1,128,128]{2,1,0:T(8,128)}) fusion(f32[1,128,128]{2,1,0:T(8,128)S(1)} %copy-done, f32[128]{0:T(128)S(1)} %bitcast.8, f32[1,128,128]{2,1,0:T(8,128)S(1)} %copy-done.1, f32[1,128,128]{2,1,0:T(8,128)S(1)} %get-tuple-element.7, f32[128]{0:T(128)S(1)} %bitcast.7, ...), kind=kLoop, calls=%fused_computation | loop fusion | flops 98304 | bytes 459776 | tf_op jit(solution)/shard_map/add | solution.py:704
Async XLA Ops:
  1.3 29.1 %copy-start = (f32[1,128,128]{2,1,0:T(8,128)S(1)}, f32[1,128,128]{2,1,0:T(8,128)}, u32[]{:S(2)}) copy-start(f32[1,128,128]{2,1,0:T(8,128)} %refs_0_.1) | copy-start | bytes 196612
  1.3 29.1 %copy-start.1 = (f32[1,128,128]{2,1,0:T(8,128)S(1)}, f32[1,128,128]{2,1,0:T(8,128)}, u32[]{:S(2)}) copy-start(f32[1,128,128]{2,1,0:T(8,128)} %refs_13_.1) | copy-start | bytes 196612
  1.3 29.1 %copy-start.2 = (f32[1,128,128]{2,1,0:T(8,128)S(1)}, f32[1,128,128]{2,1,0:T(8,128)}, u32[]{:S(2)}) copy-start(f32[1,128,128]{2,1,0:T(8,128)} %param.15) | copy-start | bytes 196612

commit v2 on v1

--- a/solution.py
+++ b/solution.py
@@ -196,14 +196,6 @@
     return max(2, (2 * slots + panels - 1) // panels)
 
 
-def place(flat, tiles, levs, subs):
-    return {
-        "tile": flat // (levs * subs),
-        "lev": (flat // subs) % levs,
-        "sub": flat % subs,
-    }
-
-
 def hail(peers):
     barrier = pltpu.get_barrier_semaphore()
     for peer in peers:
@@ -215,10 +207,24 @@
 
 
 def group_peers(sizes):
-    tiles, levs, subs = sizes
-    total = tiles * levs * subs
-    me = (lax.axis_index("tile") * levs + lax.axis_index("lev")) * subs + lax.axis_index("sub")
-    return [place(lax.rem(me + k, total), *sizes) for k in range(1, total)]
+    axes = ("tile", "lev", "sub")
+    steps = [(t, l, u) for t in range(sizes[0]) for l in range(sizes[1]) for u in range(sizes[2])]
+    steps.sort(key=lambda d: (-min(d[0], sizes[0] - d[0]), -d[1], -d[2]))
+    return [
+        {axis: lax.rem(lax.axis_index(axis) + by, size) for axis, by, size in zip(axes, d, sizes)}
+        for d in steps if any(d)
+    ]
+
+
+def by_distance(tile, tiles):
+    table = [sorted((t for t in range(tiles) if t != me), key=lambda t: abs(t - me)) for me in range(tiles)]
+    picks = []
+    for k in range(tiles - 1):
+        pick = jnp.int32(table[0][k])
+        for me in range(1, tiles):
+            pick = jnp.where(tile == me, table[me][k], pick)
+        picks.append(pick)
+    return picks
 
 
 def dot(a, b, dims, precision=None):
@@ -299,49 +305,39 @@
     return (q[2], q[3], q[0], q[1])
 
 
-def pairing_matrix(pair_ref, flip_ref, panels):
+def turned(x):
+    width = x.shape[1]
+    back = width - 1 - iota((8, width), 1)
+    return jnp.concatenate(
+        [jnp.take_along_axis(x[r : r + 8], back, axis=1) for r in range(0, x.shape[0], 8)], axis=0)
+
+
+def partner_rows(pair_ref, flip_ref, levels, panels):
     sides = 4 * panels
-    pair, turned = pair_ref[...].T, flip_ref[...].T
-    code = (pair % 4) * panels + pair // 4 + sides * turned
-    code = jnp.concatenate([code[:, k : k + 1] for k in range(4)], axis=0)
-    shape = (sides, 2 * sides)
-    picks = code == iota(shape, 1)
-    return jnp.concatenate([picks.astype(F32)] * 2, axis=1).astype(BF16)
-
-
-def reversal(width):
-    shape = (2 * width, width)
-    a = iota(shape, 0)
-    a = jnp.where(a < width, a, a - width)
-    return (a + iota(shape, 1) == width - 1).astype(BF16)
-
-
-def exchange(strips, choose, rev):
+
+    def row(k, p):
+        pair = pair_ref[k, p]
+        return (flip_ref[k, p] * levels * sides) + (pair % 4) * panels + pair // 4
+
+    return row
+
+
+def exchange(strips, store, row, panel):
     levels, panels, _, width = strips[0].shape
     sides = 4 * panels
     s = jnp.concatenate(
         [strips[k][l].reshape(panels, width) for l in range(levels) for k in range(4)], axis=0)
-    high, low = halves(s)
-    turned = dot(jnp.concatenate([high, low], axis=1).astype(BF16), rev, NN)
-    thigh, tlow = halves(turned)
-    both = jnp.concatenate(
-        [
-            jnp.concatenate([v[l * sides : (l + 1) * sides] for v in (high, thigh, low, tlow)], axis=0)
-            for l in range(levels)
-        ], axis=1)
-    h = dot(choose, both.astype(BF16), NN)
-    return [
-        jnp.stack([
-            h[k * panels : (k + 1) * panels, l * width : (l + 1) * width] for l in range(levels)
-        ]).reshape(levels, panels, 1, width)
+    store[: levels * sides] = s
+    store[levels * sides :] = turned(s)
+
+    def strip(k, p, l):
+        return store[pl.ds(row(k, p) + l * sides, 1), :]
+
+    every = [
+        jnp.stack([jnp.stack([strip(k, p, l) for p in range(panels)]) for l in range(levels)])
         for k in range(4)
     ]
-
-
-def own_halos(h, store, panel):
-    for k in range(4):
-        store[k] = h[k].reshape(store.shape[1:])
-    return [store[k, :, pl.ds(panel, 1), :] for k in range(4)]
+    return every, [jnp.stack([strip(k, panel, l) for l in range(levels)]) for k in range(4)]
 
 
 def slot_rows(col, when, count, panels, area, width, capacity):
@@ -382,10 +378,12 @@
     loads = [
         pltpu.make_async_copy(src, dst, landed.at[k]) for k, (src, dst) in enumerate(zip(inputs, held))
     ]
+    flat_peers = group_peers(sizes)
+    near = [{axis: lax.rem(lax.axis_index(axis) + k, size)}
+            for axis, size in zip(("tile", "lev", "sub"), sizes) for k in range(1, size)]
+    hail(near)
     for load in loads[:6]:
         load.start()
-    flat_peers = group_peers(sizes)
-    hail(flat_peers)
     for load in loads[6:]:
         load.start()
 
@@ -423,45 +421,47 @@
     facts, spread = slot_rows(
         col_ref[...], time_ref[...], count_ref[0], panels, area, width, capacity)
     bands[lev, panel, base : base + FACTS] = facts[:FACTS]
-    hailed(flat_peers)
+    hailed(near)
     started = []
 
-    def send(src, dst, ssem, rsem, where):
-        copy = pltpu.make_async_remote_copy(
+    def remote(src, dst, ssem, rsem, where):
+        return pltpu.make_async_remote_copy(
             src_ref=src, dst_ref=dst, send_sem=ssem, recv_sem=rsem,
             device_id=where, device_id_type=MESH)
+
+    def send(src, dst, ssem, rsem, where):
+        copy = remote(src, dst, ssem, rsem, where)
         copy.start()
         started.append(copy)
         return copy
 
-    def block(m, j):
-        return bands.at[lax.rem(lev - m + levs, levs), lax.rem(tile - j + tiles, tiles) * subs + sub]
-
-    arrivals_z, arrivals_x, arrivals_c = {}, {}, []
+    def block(level, at):
+        return bands.at[level, at * subs + sub]
+
+    arrivals_x, arrivals_c = [], []
     across = {"lev": other}
 
-    def to_subs(m, j):
+    def to_subs(level, at, k):
         for q in range(1, subs):
-            arrivals_c.append(send(block(m, j), block(m, j), csend.at[q, m, j], crecv.at[q, m, j],
+            arrivals_c.append(send(block(level, at), block(level, at), csend.at[q, level, k], crecv.at[q, level, at],
                                    {"sub": lax.rem(sub + q, subs)}))
 
-    def to_lev(j):
-        arrivals_x[j] = send(block(0, j), block(0, j), xsend.at[j], xrecv.at[j], across)
-
-    order = sorted(range(1, tiles), key=lambda k: min(k, tiles - k))
-    for k in order:
-        arrivals_z[k] = send(block(0, 0), block(0, 0), zsend.at[k], zrecv.at[k],
-                             {"tile": lax.rem(tile + k, tiles)})
-    to_lev(0)
-    to_subs(0, 0)
+    def to_lev(at, k):
+        arrivals_x.append(send(block(lev, at), block(lev, at), xsend.at[k], xrecv.at[at], across))
+
+    order = by_distance(tile, tiles)
+    sends = list(enumerate(order))[::-1]
+    for k, at in sends:
+        send(block(lev, tile), block(lev, tile), zsend.at[k], zrecv.at[tile], {"tile": at})
+    to_lev(tile, 0)
+    to_subs(lev, tile, 0)
     fields = send(stage.at[:, pl.ds(ostart, rows)], win.at[lev], fsend, frecv, across)
     for f in range(3):
         win[lev, f] = stage[f, pl.ds(start, rows)]
     for load in loads[6:]:
         load.wait()
     jmine[...] = jac_ref[...].astype(F32)
-    choose = pairing_matrix(pair_ref, flip_ref, panels)
-    rev = reversal(width)
+    partner = partner_rows(pair_ref, flip_ref, levs, panels)
     e8 = jnp.broadcast_to(err_ref[...][None, :], (8, channels))
     high = lax.Precision.HIGHEST
 
@@ -472,17 +472,21 @@
         return out[:1] + out[8:9]
 
     gall[lev, panel, 0:1] = slotted(dot(e8, jmine[...] * jmine[...], NT, high))
-    for k in order:
-        arrivals_z[k].wait_recv()
-        to_lev(k)
-        to_subs(0, k)
+    for k, at in enumerate(order):
+        remote(block(lev, at), block(lev, at), zsend.at[k], zrecv.at[at], {"tile": at}).wait_recv()
+        to_lev(at, k + 1)
+        to_subs(lev, at, k + 1)
     jcopy = send(jmine.at[pl.ds(pl.multiple_of(other * share, MARGIN), share)], jother, jsend, jrecv, across)
-    rcopy = send(res_ref.at[0, pl.ds(omid, half)], rother, rsend, rrecv, across)
-    for j in [0] + order:
-        arrivals_x[j].wait_recv()
-        to_subs(1, j)
-    for copy in [fields] + arrivals_c:
-        copy.wait_recv()
+    for k, at in enumerate([tile] + order):
+        remote(block(other, at), block(other, at), xsend.at[k], xrecv.at[at], across).wait_recv()
+        to_subs(other, at, k)
+    fields.wait_recv()
+    for level in (lev, other):
+        for q in range(1, subs):
+            for at in [tile] + order:
+                whence = bands.at[level, at * subs + lax.rem(sub + q, subs)]
+                remote(whence, whence, csend.at[q, level, 0], crecv.at[q, level, at],
+                       {"sub": lax.rem(sub + q, subs)}).wait_recv()
 
     def band(f, which):
         at = (2 * f + which) * tips
@@ -513,8 +517,7 @@
     picked = [None] * levs
     for step in range(STEPS):
         strips = (x_ns[:, :, :1], x_ns[:, :, last:], x_we[:, :, :1], x_we[:, :, last:])
-        h = exchange(strips, choose, rev)
-        ho = own_halos(h, store.at[step % 2], panel)
+        h, ho = exchange(strips, store.at[step % 2], partner, panel)
         x = forward_tile(x, own, *scal3, ho, hit3)
         if step + 1 < STEPS:
             x_ns, x_we = (
@@ -544,6 +547,7 @@
         for k, where in enumerate(flat_peers)
     ]
 
+    rcopy = send(res_ref.at[0, pl.ds(omid, half)], rother, rsend, rrecv, across)
     edge = edge_index((tips, width), tips, width).astype(F32) + 1.0
     spots = fiota((width, width), 0) + 1.0
 
@@ -601,8 +605,7 @@
         p_ns = [c * x_ns for c in ns]
         p_we = [c * x_we for c in we]
         strips = (p_ns[0][:, :, :1], p_ns[1][:, :, last:], p_we[0][:, :, :1], p_we[1][:, :, last:])
-        h = exchange(strips, choose, rev)
-        ho = own_halos(h, store.at[step % 2], panel)
+        h, ho = exchange(strips, store.at[step % 2], partner, panel)
         x = adjoint_tile(x, [c * x for c in own], *scal3, ho, hit3)
         if step > 0:
             x = x + force[step - 1]
@@ -660,7 +663,7 @@
         jacobian.reshape(slots, channels), error_inv, side_pair.T, side_flip.T, diffusion, vertical,
         background_inv, residual,
     )
-    scalars = (5, 10, 11, 12)
+    scalars = (5, 8, 9, 10, 11, 12)
     landing = [
         (pltpu.SMEM if k in scalars else pltpu.VMEM)(x.shape, x.dtype) for k, x in enumerate(inputs)
     ]
@@ -683,7 +686,7 @@
             pltpu.VMEM((half, width), F32),
             pltpu.VMEM((half, width), F32),
             pltpu.VMEM((half, width), F32),
-            pltpu.VMEM((2, 4, levs, panels, width), F32),
+            pltpu.VMEM((2, 2 * levs * 4 * panels, width), F32),
             pltpu.VMEM((FACTS, panels, width), F32),
             dma, dma,
             dma((tiles,)), dma((tiles,)),

time: 31.2 us -> 29.8 us (0.955)
  Pallas kernels: 29 us -> 27.6 us
    pallas_call x1, Pallas kernels: 29 us -> 27.6 us  [fused_body(): pl.pallas_call(functools.partial(whole_kernel, sizes, slot_capacity(slots...]
where the time goes in v2:
time: 29.8 us; the launch traced here: 29.6 us
  Pallas kernels  27.6 us (93%)
  between operations  1.34 us (4%)
  other arithmetic  0.69 us (2%)
    pallas_call x1, Pallas kernels, fused_body(): pl.pallas_call(functools.partial(whole_kernel, sizes, slot_capacity(slots...  27.6 us
    add x1, other arithmetic, fused_body(): return (increment + alpha * direction, left, left + beta * direction)  0.69 us

profile of v2, /device:TPU:0, one launch (start us, length us, event | category | flops | bytes accessed | tf_op | source)
XLA Modules:
  0.0 29.6 jit_solution(2406710654046259903)
XLA Ops:
  1.3 0.0 copy-start
  1.3 0.0 copy-start.1
  1.3 0.0 copy-start.2
  1.3 27.6 %whole.1 = (f32[1,128,128]{2,1,0:T(8,128)S(1)}, f32[1,1,128]{2,1,0:T(1,128)S(1)}, f32[1,1,128]{2,1,0:T(1,128)S(1)}) custom-call(f32[1,128,128]{2,1,0:T(8,128)} %refs_0_.1, bf16[1,128,128]{2,1,0:T(8,128)(2,1)} %refs_1_.1, bf16[1,128,128]{2,1,0:T(8,128)(2,1)} %refs_2_.1, s32[1,64]{1,0:T(1,128)} %bitcast.12, s32[1,64]{1,0:T(1,128)} %bitcast.13, ...), custom_call_target="tpu_custom_call" | custom-call | tf_op jit(solution)/shard_map/whole/pallas_call | solution.py:671
  28.9 0.0 copy-done
  28.9 0.0 copy-done.1
  28.9 0.0 copy-done.2
  28.9 0.7 %multiply_add_fusion = (f32[1,128,128]{2,1,0:T(8,128)}, f32[1,128,128]{2,1,0:T(8,128)}, f32[1,128,128]{2,1,0:T(8,128)}) fusion(f32[1,128,128]{2,1,0:T(8,128)S(1)} %copy-done, f32[128]{0:T(128)S(1)} %bitcast.8, f32[1,128,128]{2,1,0:T(8,128)S(1)} %copy-done.1, f32[1,128,128]{2,1,0:T(8,128)S(1)} %get-tuple-element.7, f32[128]{0:T(128)S(1)} %bitcast.7, ...), kind=kLoop, calls=%fused_computation | loop fusion | flops 98304 | bytes 459776 | tf_op jit(solution)/shard_map/add | solution.py:707
Async XLA Ops:
  1.3 27.6 %copy-start = (f32[1,128,128]{2,1,0:T(8,128)S(1)}, f32[1,128,128]{2,1,0:T(8,128)}, u32[]{:S(2)}) copy-start(f32[1,128,128]{2,1,0:T(8,128)} %refs_0_.1) | copy-start | bytes 196612
  1.3 27.6 %copy-start.1 = (f32[1,128,128]{2,1,0:T(8,128)S(1)}, f32[1,128,128]{2,1,0:T(8,128)}, u32[]{:S(2)}) copy-start(f32[1,128,128]{2,1,0:T(8,128)} %refs_13_.1) | copy-start | bytes 196612
  1.3 27.6 %copy-start.2 = (f32[1,128,128]{2,1,0:T(8,128)S(1)}, f32[1,128,128]{2,1,0:T(8,128)}, u32[]{:S(2)}) copy-start(f32[1,128,128]{2,1,0:T(8,128)} %param.15) | copy-start | bytes 196612

commit v3 on v2

--- a/solution.py
+++ b/solution.py
@@ -352,7 +352,9 @@
     spread = (fiota((panels * capacity, slots), 0) == slot).astype(BF16)
     facts = jnp.concatenate([cell // width + 1, cell % width + 1, when], axis=0).astype(F32)
     facts = jnp.concatenate([facts, jnp.zeros((8 - FACTS, slots), F32)], axis=0)
-    return dot(facts.astype(BF16), spread, NT), spread
+    tall = jnp.concatenate([slot, jnp.zeros((7, slots), F32)], axis=0).T
+    upright = (fiota((slots, panels * capacity), 1) == tall[:, 0:1]).astype(F32)
+    return dot(facts.astype(BF16), spread, NT), spread, upright
 
 
 def by_panel(a, capacity):
@@ -370,7 +372,7 @@
     tiles, levs, subs = sizes
     inputs, (img_out, alpha_out, beta_out) = refs[:INPUTS], refs[INPUTS : INPUTS + 3]
     held = refs[INPUTS + 3 : 2 * INPUTS + 3]
-    (landed, stage, win, bands, jmine, jother, gall, vall, sall, rother, isent, igot, store, box,
+    (landed, stage, win, bands, jmine, jother, gall, vall, sall, rother, isent, igot, store, box, upright,
      fsend, frecv, zsend, zrecv, xsend, xrecv, csend, crecv, jsend, jrecv, rsend, rrecv, isend, irecv,
      gsend, grecv, vsend, vrecv, ssend, srecv) = refs[2 * INPUTS + 3 :]
     (dir_ref, wu_ref, wv_ref, col_ref, time_ref, count_ref, jac_ref, err_ref, pair_ref, flip_ref,
@@ -418,7 +420,7 @@
         bands[lev, panel, at + tips + STEPS : at + 2 * tips] = xt[width - STEPS :]
     for load in loads[3:6]:
         load.wait()
-    facts, spread = slot_rows(
+    facts, spread, upright[...] = slot_rows(
         col_ref[...], time_ref[...], count_ref[0], panels, area, width, capacity)
     bands[lev, panel, base : base + FACTS] = facts[:FACTS]
     hailed(near)
@@ -476,17 +478,30 @@
         remote(block(lev, at), block(lev, at), zsend.at[k], zrecv.at[at], {"tile": at}).wait_recv()
         to_lev(at, k + 1)
         to_subs(lev, at, k + 1)
-    jcopy = send(jmine.at[pl.ds(pl.multiple_of(other * share, MARGIN), share)], jother, jsend, jrecv, across)
-    for k, at in enumerate([tile] + order):
-        remote(block(other, at), block(other, at), xsend.at[k], xrecv.at[at], across).wait_recv()
-        to_subs(other, at, k)
-    fields.wait_recv()
-    for level in (lev, other):
+
+    def from_sub(level):
         for q in range(1, subs):
             for at in [tile] + order:
                 whence = bands.at[level, at * subs + lax.rem(sub + q, subs)]
                 remote(whence, whence, csend.at[q, level, 0], crecv.at[q, level, at],
                        {"sub": lax.rem(sub + q, subs)}).wait_recv()
+
+    from_sub(lev)
+    jcopy = send(jmine.at[pl.ds(pl.multiple_of(other * share, MARGIN), share)], jother, jsend, jrecv, across)
+    for k, at in enumerate([tile] + order):
+        remote(block(other, at), block(other, at), xsend.at[k], xrecv.at[at], across).wait_recv()
+        to_subs(other, at, k)
+
+    o_i, o_j, o_t = [by_panel(bands[lev, :, base + k, :], capacity) for k in range(FACTS)]
+    for k, v in enumerate((o_i, o_j, o_t)):
+        box[k] = v
+    s_i, s_j, s_t = [box[k, pl.ds(panel, 1), :] for k in range(FACTS)]
+    line = iota((rows, width), 0)
+    mine = (line + start + 1).astype(F32) == s_i
+    inside = jnp.where((line >= lev * MARGIN) & (line < lev * MARGIN + half), 1.0, 0.0)
+    here = jnp.where(mine, inside, 0.0)
+    fields.wait_recv()
+    from_sub(other)
 
     def band(f, which):
         at = (2 * f + which) * tips
@@ -506,15 +521,10 @@
     hit3 = iota((rows, width), 0) + start == iota((rows, width), 1)
     x_ns, x_we, x = band(0, 0), band(0, 1), win[:, 0]
 
-    o_i, o_j, o_t = [by_panel(bands[0, :, base + k, :], capacity) for k in range(FACTS)]
-    for k, v in enumerate((o_i, o_j, o_t)):
-        box[k] = v
-    s_i, s_j, s_t = [box[k, pl.ds(panel, 1), :] for k in range(FACTS)]
-    line = iota((rows, width), 0)
-    mine = (line + start + 1).astype(F32) == s_i
-    inside = jnp.where((line >= lev * MARGIN) & (line < lev * MARGIN + half), 1.0, 0.0)
-    here = jnp.where(mine, inside, 0.0)
-    picked = [None] * levs
+    at_j = fiota((width, width), 0) + 1.0 == s_j
+    pick_j = jnp.where(at_j, 1.0, 0.0)
+    pick_j = jnp.concatenate([pick_j, pick_j], axis=0).astype(BF16)
+    picked = jnp.zeros((levs, rows, width), F32)
     for step in range(STEPS):
         strips = (x_ns[:, :, :1], x_ns[:, :, last:], x_we[:, :, :1], x_we[:, :, last:])
         h, ho = exchange(strips, store.at[step % 2], partner, panel)
@@ -525,23 +535,20 @@
                 forward_tile(x_we, we, *scal4, swap(h), hit4),
             )
         now = jnp.where(s_t == step + 1.0, here, 0.0)
-        now = jnp.concatenate([now, now], axis=0).astype(BF16)
-        for l in range(levs):
-            got = dot(jnp.concatenate(halves(x[l]), axis=0).astype(BF16), now, TN)
-            picked[l] = got if picked[l] is None else picked[l] + got
+        both = jnp.concatenate([jnp.concatenate(halves(x[l]), axis=1) for l in range(levs)], axis=0)
+        picked = picked + now * dot(both.astype(BF16), pick_j, NN).reshape(levs, rows, width)
         if step == 1:
             jcopy.wait_recv()
-            cross = dot(e8, jmine[pl.ds(pl.multiple_of(lev * share, MARGIN), share)] * jother[...], NT, high)
-            cross = jnp.concatenate([cross] * levs, axis=1)
-            cross = jnp.where(iota(cross.shape, 1) // share == lev, cross, 0.0)
-            gall[lev, panel, 1:2] = slotted(cross)
+            near_half = pl.multiple_of(lev * share, MARGIN)
+            cross = jmine[pl.ds(near_half, share)] * jother[...] * err_ref[...][None, :]
+            cross = jnp.sum(cross, axis=1, keepdims=True) * upright[pl.ds(near_half, share)]
+            gall[lev, panel, 1:2] = jnp.sum(cross, axis=0, keepdims=True)
             arrivals_g = [
                 send(gall.at[lev, panel], gall.at[lev, panel], gsend.at[k], grecv.at[k], where)
                 for k, where in enumerate(flat_peers)
             ]
-    at_j = fiota((width, width), 0) + 1.0 == s_j
     for l in range(levs):
-        vall[lev, panel, l : l + 1] = jnp.sum(jnp.where(at_j, picked[l], 0.0), axis=0, keepdims=True)
+        vall[lev, panel, l : l + 1] = jnp.sum(picked[l], axis=0, keepdims=True)
     arrivals_v = [
         send(vall.at[lev, panel], vall.at[lev, panel], vsend.at[k], vrecv.at[k], where)
         for k, where in enumerate(flat_peers)
@@ -624,6 +631,7 @@
         part = jnp.concatenate([jnp.sum(a * b, axis=0, keepdims=True) for a, b in pairs], axis=0)
         sums = part if sums is None else sums + part
     sall[me] = sums
+    before = list(started)
     arrivals_s = [
         send(sall.at[me], sall.at[me], ssend.at[k], srecv.at[k], where)
         for k, where in enumerate(flat_peers)
@@ -631,6 +639,8 @@
     isent[...] = jnp.where(lev == 0, image[1], image[0])
     icopy = send(isent, igot, isend, irecv, across)
     img_out[0, pl.ds(mid, half)] = jnp.where(lev == 0, image[0], image[1])
+    for copy in before:
+        copy.wait_send()
     icopy.wait_recv()
     img_out[0, pl.ds(omid, half)] = igot[...]
     for copy in arrivals_s:
@@ -641,7 +651,7 @@
     new = old - 2.0 * alpha * cross + alpha * alpha * square
     alpha_out[0] = jnp.broadcast_to(alpha, alpha_out.shape[1:])
     beta_out[0] = jnp.broadcast_to(new / old, beta_out.shape[1:])
-    for copy in started:
+    for copy in started[len(before) :]:
         copy.wait_send()
 
 
@@ -688,6 +698,7 @@
             pltpu.VMEM((half, width), F32),
             pltpu.VMEM((2, 2 * levs * 4 * panels, width), F32),
             pltpu.VMEM((FACTS, panels, width), F32),
+            pltpu.VMEM((slots, width), F32),
             dma, dma,
             dma((tiles,)), dma((tiles,)),
             dma((tiles,)), dma((tiles,)),

time: 29.8 us -> 29.5 us (0.990)
  Pallas kernels: 27.6 us -> 27.3 us
where the time goes in v3:
time: 29.5 us; the launch traced here: 29.3 us
  Pallas kernels  27.3 us (93%)
  between operations  1.34 us (5%)
  other arithmetic  0.69 us (2%)
    pallas_call x1, Pallas kernels, fused_body(): pl.pallas_call(functools.partial(whole_kernel, sizes, slot_capacity(slots...  27.3 us
    add x1, other arithmetic, fused_body(): return (increment + alpha * direction, left, left + beta * direction)  0.69 us

profile of v3, /device:TPU:0, one launch (start us, length us, event | category | flops | bytes accessed | tf_op | source)
XLA Modules:
  0.0 29.3 jit_solution(11412377739258791497)
XLA Ops:
  1.3 0.0 copy-start
  1.3 0.0 copy-start.1
  1.3 0.0 copy-start.2
  1.3 27.3 %whole.1 = (f32[1,128,128]{2,1,0:T(8,128)S(1)}, f32[1,1,128]{2,1,0:T(1,128)S(1)}, f32[1,1,128]{2,1,0:T(1,128)S(1)}) custom-call(f32[1,128,128]{2,1,0:T(8,128)} %refs_0_.1, bf16[1,128,128]{2,1,0:T(8,128)(2,1)} %refs_1_.1, bf16[1,128,128]{2,1,0:T(8,128)(2,1)} %refs_2_.1, s32[1,64]{1,0:T(1,128)} %bitcast.12, s32[1,64]{1,0:T(1,128)} %bitcast.13, ...), custom_call_target="tpu_custom_call" | custom-call | tf_op jit(solution)/shard_map/whole/pallas_call | solution.py:681
  28.6 0.0 copy-done
  28.6 0.0 copy-done.1
  28.6 0.0 copy-done.2
  28.6 0.7 %multiply_add_fusion = (f32[1,128,128]{2,1,0:T(8,128)}, f32[1,128,128]{2,1,0:T(8,128)}, f32[1,128,128]{2,1,0:T(8,128)}) fusion(f32[1,128,128]{2,1,0:T(8,128)S(1)} %copy-done, f32[128]{0:T(128)S(1)} %bitcast.8, f32[1,128,128]{2,1,0:T(8,128)S(1)} %copy-done.1, f32[1,128,128]{2,1,0:T(8,128)S(1)} %get-tuple-element.7, f32[128]{0:T(128)S(1)} %bitcast.7, ...), kind=kLoop, calls=%fused_computation | loop fusion | flops 98304 | bytes 459776 | tf_op jit(solution)/shard_map/add | solution.py:718
Async XLA Ops:
  1.3 27.3 %copy-start = (f32[1,128,128]{2,1,0:T(8,128)S(1)}, f32[1,128,128]{2,1,0:T(8,128)}, u32[]{:S(2)}) copy-start(f32[1,128,128]{2,1,0:T(8,128)} %refs_0_.1) | copy-start | bytes 196612
  1.3 27.3 %copy-start.1 = (f32[1,128,128]{2,1,0:T(8,128)S(1)}, f32[1,128,128]{2,1,0:T(8,128)}, u32[]{:S(2)}) copy-start(f32[1,128,128]{2,1,0:T(8,128)} %refs_13_.1) | copy-start | bytes 196612
  1.3 27.3 %copy-start.2 = (f32[1,128,128]{2,1,0:T(8,128)S(1)}, f32[1,128,128]{2,1,0:T(8,128)}, u32[]{:S(2)}) copy-start(f32[1,128,128]{2,1,0:T(8,128)} %param.15) | copy-start | bytes 196612

commit v4 on v3

--- a/solution.py
+++ b/solution.py
@@ -437,8 +437,12 @@
         started.append(copy)
         return copy
 
-    def block(level, at):
-        return bands.at[level, at * subs + sub]
+    def block(level, at, by=0):
+        index = at * subs + lax.rem(sub + by, subs)
+        return bands.at[level, index] if level is lev else bands.at[level, index, pl.ds(0, base)]
+
+    def across_block(level, at):
+        return bands.at[level, at * subs + sub, pl.ds(0, base)]
 
     arrivals_x, arrivals_c = [], []
     across = {"lev": other}
@@ -449,7 +453,7 @@
                                    {"sub": lax.rem(sub + q, subs)}))
 
     def to_lev(at, k):
-        arrivals_x.append(send(block(lev, at), block(lev, at), xsend.at[k], xrecv.at[at], across))
+        arrivals_x.append(send(across_block(lev, at), across_block(lev, at), xsend.at[k], xrecv.at[at], across))
 
     order = by_distance(tile, tiles)
     sends = list(enumerate(order))[::-1]
@@ -482,14 +486,14 @@
     def from_sub(level):
         for q in range(1, subs):
             for at in [tile] + order:
-                whence = bands.at[level, at * subs + lax.rem(sub + q, subs)]
+                whence = block(level, at, q)
                 remote(whence, whence, csend.at[q, level, 0], crecv.at[q, level, at],
                        {"sub": lax.rem(sub + q, subs)}).wait_recv()
 
     from_sub(lev)
     jcopy = send(jmine.at[pl.ds(pl.multiple_of(other * share, MARGIN), share)], jother, jsend, jrecv, across)
     for k, at in enumerate([tile] + order):
-        remote(block(other, at), block(other, at), xsend.at[k], xrecv.at[at], across).wait_recv()
+        remote(across_block(other, at), across_block(other, at), xsend.at[k], xrecv.at[at], across).wait_recv()
         to_subs(other, at, k)
 
     o_i, o_j, o_t = [by_panel(bands[lev, :, base + k, :], capacity) for k in range(FACTS)]
@@ -537,7 +541,7 @@
         now = jnp.where(s_t == step + 1.0, here, 0.0)
         both = jnp.concatenate([jnp.concatenate(halves(x[l]), axis=1) for l in range(levs)], axis=0)
         picked = picked + now * dot(both.astype(BF16), pick_j, NN).reshape(levs, rows, width)
-        if step == 1:
+        if step == 2:
             jcopy.wait_recv()
             near_half = pl.multiple_of(lev * share, MARGIN)
             cross = jmine[pl.ds(near_half, share)] * jother[...] * err_ref[...][None, :]

time: 29.5 us -> 28.8 us (0.976)
  Pallas kernels: 27.3 us -> 26.6 us
    pallas_call x1, Pallas kernels: 27.3 us -> 26.6 us  [fused_body(): pl.pallas_call(functools.partial(whole_kernel, sizes, slot_capacity(slots...]
where the time goes in v4:
time: 28.8 us; the launch traced here: 28.7 us
  Pallas kernels  26.6 us (92%)
  between operations  1.34 us (5%)
  other arithmetic  0.69 us (2%)
    pallas_call x1, Pallas kernels, fused_body(): pl.pallas_call(functools.partial(whole_kernel, sizes, slot_capacity(slots...  26.6 us
    add x1, other arithmetic, fused_body(): return (increment + alpha * direction, left, left + beta * direction)  0.69 us

profile of v4, /device:TPU:0, one launch (start us, length us, event | category | flops | bytes accessed | tf_op | source)
XLA Modules:
  0.0 28.7 jit_solution(9286086604552980409)
XLA Ops:
  1.3 0.0 copy-start
  1.3 0.0 copy-start.1
  1.3 0.0 copy-start.2
  1.3 26.6 %whole.1 = (f32[1,128,128]{2,1,0:T(8,128)S(1)}, f32[1,1,128]{2,1,0:T(1,128)S(1)}, f32[1,1,128]{2,1,0:T(1,128)S(1)}) custom-call(f32[1,128,128]{2,1,0:T(8,128)} %refs_0_.1, bf16[1,128,128]{2,1,0:T(8,128)(2,1)} %refs_1_.1, bf16[1,128,128]{2,1,0:T(8,128)(2,1)} %refs_2_.1, s32[1,64]{1,0:T(1,128)} %bitcast.12, s32[1,64]{1,0:T(1,128)} %bitcast.13, ...), custom_call_target="tpu_custom_call" | custom-call | tf_op jit(solution)/shard_map/whole/pallas_call | solution.py:685
  27.9 0.0 copy-done
  28.0 0.0 copy-done.1
  28.0 0.0 copy-done.2
  28.0 0.7 %multiply_add_fusion = (f32[1,128,128]{2,1,0:T(8,128)}, f32[1,128,128]{2,1,0:T(8,128)}, f32[1,128,128]{2,1,0:T(8,128)}) fusion(f32[1,128,128]{2,1,0:T(8,128)S(1)} %copy-done, f32[128]{0:T(128)S(1)} %bitcast.8, f32[1,128,128]{2,1,0:T(8,128)S(1)} %copy-done.1, f32[1,128,128]{2,1,0:T(8,128)S(1)} %get-tuple-element.7, f32[128]{0:T(128)S(1)} %bitcast.7, ...), kind=kLoop, calls=%fused_computation | loop fusion | flops 98304 | bytes 459776 | tf_op jit(solution)/shard_map/add | solution.py:722
Async XLA Ops:
  1.3 26.7 %copy-start = (f32[1,128,128]{2,1,0:T(8,128)S(1)}, f32[1,128,128]{2,1,0:T(8,128)}, u32[]{:S(2)}) copy-start(f32[1,128,128]{2,1,0:T(8,128)} %refs_0_.1) | copy-start | bytes 196612
  1.3 26.7 %copy-start.1 = (f32[1,128,128]{2,1,0:T(8,128)S(1)}, f32[1,128,128]{2,1,0:T(8,128)}, u32[]{:S(2)}) copy-start(f32[1,128,128]{2,1,0:T(8,128)} %refs_13_.1) | copy-start | bytes 196612
  1.3 26.7 %copy-start.2 = (f32[1,128,128]{2,1,0:T(8,128)S(1)}, f32[1,128,128]{2,1,0:T(8,128)}, u32[]{:S(2)}) copy-start(f32[1,128,128]{2,1,0:T(8,128)} %param.15) | copy-start | bytes 196612
